TPU v7x, 8 devices: a whole 2x2x1 slice. The times are simulated.
8 devices in a mesh: stage: 4 (over z, y, x), data: 2 (over core).
Axes of the slice: x: 2, y: 2, z: 1, core: 2. Of those that a mesh axis runs over, the one named last changes fastest.
Arguments:
- inputs: bfloat16 [8, 1024, 2048], P('data')
- targets: bfloat16 [8, 1024, 2048], P('data')
- w_up: bfloat16 [4, 2048, 8192], P('stage')
- w_down: bfloat16 [4, 8192, 2048], P('stage')
Outputs:
- output 1: float32 [], replicated
- output 2: float32 [4, 2048, 8192], P('stage', 'data')
- output 3: float32 [4, 8192, 2048], P('stage', None, 'data')
All inputs are finite; a program needn't handle non-finite values.
Results may differ from a plain program's by a relative error of at most 0.00277113.
Values are sent between devices in bfloat16 or wider.
A program may use at most 1 GiB of HBM per device.

v0:
```python
import jax
import jax.numpy as jnp
from jax import lax
from jax.sharding import PartitionSpec as P, NamedSharding

CONTRACT_ROWS = (((0,), (0,)), ((), ()))
CONTRACT_COLS = (((1,), (1,)), ((), ()))


def layer_forward(h_in, w_up, w_down):
    pre_act = jnp.dot(h_in, w_up, preferred_element_type=jnp.float32)
    gelu_out = jax.nn.gelu(pre_act).astype(jnp.bfloat16)
    branch = jnp.dot(gelu_out, w_down, preferred_element_type=jnp.float32)
    return (h_in.astype(jnp.float32) + branch).astype(jnp.bfloat16)


def layer_backward(h_in, grad_out, w_up, w_down):
    pre_act = jnp.dot(h_in, w_up, preferred_element_type=jnp.float32)
    gelu_full, gelu_vjp = jax.vjp(jax.nn.gelu, pre_act)
    gelu_out = gelu_full.astype(jnp.bfloat16)
    g_down = lax.dot_general(gelu_out, grad_out, CONTRACT_ROWS, preferred_element_type=jnp.float32)
    grad_act = lax.dot_general(grad_out, w_down, CONTRACT_COLS, preferred_element_type=jnp.float32).astype(jnp.bfloat16)
    grad_pre = gelu_vjp(grad_act.astype(jnp.float32))[0].astype(jnp.bfloat16)
    g_up = lax.dot_general(h_in, grad_pre, CONTRACT_ROWS, preferred_element_type=jnp.float32)
    back_prod = lax.dot_general(grad_pre, w_up, CONTRACT_COLS, preferred_element_type=jnp.float32)
    grad_in = (grad_out.astype(jnp.float32) + back_prod).astype(jnp.bfloat16)
    return grad_in, g_up, g_down


def solution(mesh):
    n_stage = mesh.shape['stage']
    n_data = mesh.shape['data']
    fwd_perm = [(k, k + 1) for k in range(n_stage - 1)]
    bwd_perm = [(k + 1, k) for k in range(n_stage - 1)]

    def per_device(inputs, targets, w_up, w_down):
        n_micro, n_tok, width = inputs.shape
        n_local = w_up.shape[0]
        stage_id = lax.axis_index('stage')
        is_first = stage_id == 0
        is_last = stage_id == n_stage - 1
        n_slots = min(n_micro, 2 * n_stage)
        inv_total = 1.0 / (n_data * n_micro * n_tok)

        def run_forward(h_first):
            layer_ins = []
            h_cur = h_first
            for layer_idx in range(n_local):
                layer_ins.append(h_cur)
                h_cur = layer_forward(h_cur, w_up[layer_idx], w_down[layer_idx])
            return h_cur, jnp.stack(layer_ins)

        def skip_forward(h_first):
            return jnp.zeros_like(h_first), jnp.zeros((n_local, n_tok, width), jnp.bfloat16)

        def run_backward(operands):
            grad_cur, saved_in, acc_up, acc_down = operands
            grads_up = []
            grads_down = []
            for layer_idx in reversed(range(n_local)):
                grad_cur, g_up, g_down = layer_backward(saved_in[layer_idx], grad_cur, w_up[layer_idx], w_down[layer_idx])
                grads_up.append(g_up)
                grads_down.append(g_down)
            return grad_cur, acc_up + jnp.stack(grads_up[::-1]), acc_down + jnp.stack(grads_down[::-1])

        def skip_backward(operands):
            return jnp.zeros_like(operands[0]), operands[2], operands[3]

        def tick(tick_idx, loop_state):
            recv_fwd, recv_bwd, last_grad, stash, acc_up, acc_down, loss_sum = loop_state
            fwd_mb = tick_idx - stage_id
            fwd_ok = (fwd_mb >= 0) & (fwd_mb < n_micro)
            fwd_row = jnp.clip(fwd_mb, 0, n_micro - 1)
            x_mb = lax.dynamic_index_in_dim(inputs, fwd_row, 0, keepdims=False)
            h_first = jnp.where(is_first, x_mb, recv_fwd)
            h_out, layer_ins = lax.cond(fwd_ok, run_forward, skip_forward, h_first)
            y_mb = lax.dynamic_index_in_dim(targets, fwd_row, 0, keepdims=False)
            resid_diff = h_out.astype(jnp.float32) - y_mb.astype(jnp.float32)
            loss_sum = loss_sum + jnp.where(fwd_ok & is_last, jnp.sum(resid_diff * resid_diff), 0.0)
            top_grad = (resid_diff * inv_total).astype(jnp.bfloat16)

            bwd_mb = tick_idx - (2 * n_stage - 1 - stage_id)
            bwd_ok = (bwd_mb >= 0) & (bwd_mb < n_micro)
            bwd_slot = jnp.where(bwd_ok, bwd_mb % n_slots, n_slots)
            saved_in = lax.dynamic_index_in_dim(stash, bwd_slot, 0, keepdims=False)
            grad_first = jnp.where(is_last, last_grad, recv_bwd)
            grad_out, acc_up, acc_down = lax.cond(bwd_ok, run_backward, skip_backward, (grad_first, saved_in, acc_up, acc_down))

            fwd_slot = jnp.where(fwd_ok, fwd_mb % n_slots, n_slots)
            stash = lax.dynamic_update_index_in_dim(stash, layer_ins, fwd_slot, 0)
            recv_fwd = lax.ppermute(h_out, 'stage', fwd_perm)
            recv_bwd = lax.ppermute(grad_out, 'stage', bwd_perm)
            return recv_fwd, recv_bwd, top_grad, stash, acc_up, acc_down, loss_sum

        zero_act = jnp.zeros((n_tok, width), jnp.bfloat16)
        init_state = (zero_act, zero_act, zero_act, jnp.zeros((n_slots + 1, n_local, n_tok, width), jnp.bfloat16), jnp.zeros(w_up.shape, jnp.float32), jnp.zeros(w_down.shape, jnp.float32), jnp.zeros((), jnp.float32))
        final_state = lax.fori_loop(0, n_micro + 2 * n_stage - 1, tick, init_state)
        grad_up = lax.psum_scatter(final_state[4], 'data', scatter_dimension=1, tiled=True)
        grad_down = lax.psum_scatter(final_state[5], 'data', scatter_dimension=2, tiled=True)
        loss_total = lax.psum(final_state[6], ('stage', 'data')) * (0.5 * inv_total)
        return loss_total, grad_up, grad_down

    return jax.shard_map(per_device, mesh=mesh, in_specs=(P('data', None, None), P('data', None, None), P('stage', None, None), P('stage', None, None)), out_specs=(P(), P('stage', 'data', None), P('stage', None, 'data')), check_vma=False)
```

profile of v0, /device:TPU:3, one launch (start us, length us, event | category | flops | bytes accessed | tf_op | source)
XLA Modules:
  0.0 4088.9 jit_solution(2377964156579752647)
XLA Ops:
  62.0 3855.9 %while.28 = (s32[]{:T(128)}, bf16[1024,2048]{1,0:T(8,128)(2,1)}, bf16[1024,2048]{1,0:T(8,128)(2,1)}, bf16[1024,2048]{1,0:T(8,128)(2,1)}, bf16[5,1,1024,2048]{3,2...) while((s32[]{:T(128)}, bf16[1024,2048]{1,0:T(8,128)(2,1)}, ...), condition=%wide.region_6.7_spmd.clone, body=%wide.region_0.6_spmd.clone.sunk | while | flops 240925016064 | bytes 759170752 | solution.py:97
  76.9 92.9 %collective-permute-start.1 = (bf16[1024,2048]{1,0:T(8,128)(2,1)}, bf16[1024,2048]{1,0:T(8,128)(2,1)}, u32[]{:S(2)}, u32[]{:S(2)}) collective-permute-start(bf16[1024,2048]{1,0:T(8,128)(2,1)} %get-tuple-element.824), channel_id=1, source_target_pairs={{2,0},{4,2},{6,4},{3,1},{5,3},{7,5}} | collective-permute-start | bytes 12582920 | tf_op jit(solution)/shard_map/while/body/eval_jaxpr/ppermute | solution.py:92
  260.0 100.2 %conditional.6 = (bf16[1024,2048]{1,0:T(8,128)(2,1)}, f32[1024,2048]{1,0:T(8,128)}, bf16[1,1,1024,2048]{3,2,1,0:T(8,128)(2,1)}) conditional(s32[]{:T(128)} %convert_element_type.152, () %tuple.91, (pred[]{:T(512)}, bf16[4,1024,2048]{2,1,0:T(8,128)(2,1)}, s32[]{:T(128)}, bf16[1024,2048]{1,0:T(8,128)(2,1)}, bf16[1,2048,8192]{2,1,0:T(8,128)(2,1)}, ...), branch_computations={%region_1.1_spmd, %region_2.2_spmd} | conditional | flops 68809654272 | bytes 142607392 | solution.py:76
  383.2 70.7 %collective-permute-done = bf16[1024,2048]{1,0:T(8,128)(2,1)} collective-permute-done((bf16[1024,2048]{1,0:T(8,128)(2,1)}, bf16[1024,2048]{1,0:T(8,128)(2,1)}, u32[]{:S(2)}, u32[]{:S(2)}) %collective-permute-start) | collective-permute-done | bytes 4194336 | tf_op jit(solution)/shard_map/while/body/eval_jaxpr/ppermute | solution.py:91
  453.9 87.8 %collective-permute-done.1 = bf16[1024,2048]{1,0:T(8,128)(2,1)} collective-permute-done((bf16[1024,2048]{1,0:T(8,128)(2,1)}, bf16[1024,2048]{1,0:T(8,128)(2,1)}, u32[]{:S(2)}, u32[]{:S(2)}) %collective-permute-start.1) | collective-permute-done | bytes 4194336 | tf_op jit(solution)/shard_map/while/body/eval_jaxpr/ppermute | solution.py:92
  541.7 100.2 %conditional.6 = (bf16[1024,2048]{1,0:T(8,128)(2,1)}, f32[1024,2048]{1,0:T(8,128)}, bf16[1,1,1024,2048]{3,2,1,0:T(8,128)(2,1)}) conditional(s32[]{:T(128)} %convert_element_type.152, () %tuple.91, (pred[]{:T(512)}, bf16[4,1024,2048]{2,1,0:T(8,128)(2,1)}, s32[]{:T(128)}, bf16[1024,2048]{1,0:T(8,128)(2,1)}, bf16[1,2048,8192]{2,1,0:T(8,128)(2,1)}, ...), branch_computations={%region_1.1_spmd, %region_2.2_spmd} | conditional | flops 68809654272 | bytes 142607392 | solution.py:76
  664.9 70.1 %collective-permute-done = bf16[1024,2048]{1,0:T(8,128)(2,1)} collective-permute-done((bf16[1024,2048]{1,0:T(8,128)(2,1)}, bf16[1024,2048]{1,0:T(8,128)(2,1)}, u32[]{:S(2)}, u32[]{:S(2)}) %collective-permute-start) | collective-permute-done | bytes 4194336 | tf_op jit(solution)/shard_map/while/body/eval_jaxpr/ppermute | solution.py:91
  735.0 87.8 %collective-permute-done.1 = bf16[1024,2048]{1,0:T(8,128)(2,1)} collective-permute-done((bf16[1024,2048]{1,0:T(8,128)(2,1)}, bf16[1024,2048]{1,0:T(8,128)(2,1)}, u32[]{:S(2)}, u32[]{:S(2)}) %collective-permute-start.1) | collective-permute-done | bytes 4194336 | tf_op jit(solution)/shard_map/while/body/eval_jaxpr/ppermute | solution.py:92
  822.8 100.2 %conditional.6 = (bf16[1024,2048]{1,0:T(8,128)(2,1)}, f32[1024,2048]{1,0:T(8,128)}, bf16[1,1,1024,2048]{3,2,1,0:T(8,128)(2,1)}) conditional(s32[]{:T(128)} %convert_element_type.152, () %tuple.91, (pred[]{:T(512)}, bf16[4,1024,2048]{2,1,0:T(8,128)(2,1)}, s32[]{:T(128)}, bf16[1024,2048]{1,0:T(8,128)(2,1)}, bf16[1,2048,8192]{2,1,0:T(8,128)(2,1)}, ...), branch_computations={%region_1.1_spmd, %region_2.2_spmd} | conditional | flops 68809654272 | bytes 142607392 | solution.py:76
  946.0 69.5 %collective-permute-done = bf16[1024,2048]{1,0:T(8,128)(2,1)} collective-permute-done((bf16[1024,2048]{1,0:T(8,128)(2,1)}, bf16[1024,2048]{1,0:T(8,128)(2,1)}, u32[]{:S(2)}, u32[]{:S(2)}) %collective-permute-start) | collective-permute-done | bytes 4194336 | tf_op jit(solution)/shard_map/while/body/eval_jaxpr/ppermute | solution.py:91
  1015.5 87.8 %collective-permute-done.1 = bf16[1024,2048]{1,0:T(8,128)(2,1)} collective-permute-done((bf16[1024,2048]{1,0:T(8,128)(2,1)}, bf16[1024,2048]{1,0:T(8,128)(2,1)}, u32[]{:S(2)}, u32[]{:S(2)}) %collective-permute-start.1) | collective-permute-done | bytes 4194336 | tf_op jit(solution)/shard_map/while/body/eval_jaxpr/ppermute | solution.py:92
  1103.3 100.2 %conditional.6 = (bf16[1024,2048]{1,0:T(8,128)(2,1)}, f32[1024,2048]{1,0:T(8,128)}, bf16[1,1,1024,2048]{3,2,1,0:T(8,128)(2,1)}) conditional(s32[]{:T(128)} %convert_element_type.152, () %tuple.91, (pred[]{:T(512)}, bf16[4,1024,2048]{2,1,0:T(8,128)(2,1)}, s32[]{:T(128)}, bf16[1024,2048]{1,0:T(8,128)(2,1)}, bf16[1,2048,8192]{2,1,0:T(8,128)(2,1)}, ...), branch_computations={%region_1.1_spmd, %region_2.2_spmd} | conditional | flops 68809654272 | bytes 142607392 | solution.py:76
  1295.4 87.8 %collective-permute-done.1 = bf16[1024,2048]{1,0:T(8,128)(2,1)} collective-permute-done((bf16[1024,2048]{1,0:T(8,128)(2,1)}, bf16[1024,2048]{1,0:T(8,128)(2,1)}, u32[]{:S(2)}, u32[]{:S(2)}) %collective-permute-start.1) | collective-permute-done | bytes 4194336 | tf_op jit(solution)/shard_map/while/body/eval_jaxpr/ppermute | solution.py:92
  1392.4 119.7 %collective-permute-start = (bf16[1024,2048]{1,0:T(8,128)(2,1)}, bf16[1024,2048]{1,0:T(8,128)(2,1)}, u32[]{:S(2)}, u32[]{:S(2)}) collective-permute-start(bf16[1024,2048]{1,0:T(8,128)(2,1)} %get-tuple-element.823), channel_id=1, source_target_pairs={{0,2},{2,4},{4,6},{1,3},{3,5},{5,7}} | collective-permute-start | bytes 12582920 | tf_op jit(solution)/shard_map/while/body/eval_jaxpr/ppermute | solution.py:91
  1598.6 288.0 %collective-permute-done.1 = bf16[1024,2048]{1,0:T(8,128)(2,1)} collective-permute-done((bf16[1024,2048]{1,0:T(8,128)(2,1)}, bf16[1024,2048]{1,0:T(8,128)(2,1)}, u32[]{:S(2)}, u32[]{:S(2)}) %collective-permute-start.1) | collective-permute-done | bytes 4194336 | tf_op jit(solution)/shard_map/while/body/eval_jaxpr/ppermute | solution.py:92
  1902.9 285.2 %conditional.7 = (bf16[1024,2048]{1,0:T(8,128)(2,1)}, f32[1,2048,8192]{2,1,0:T(8,128)}, f32[1,8192,2048]{2,1,0:T(8,128)}) conditional(s32[]{:T(128)} %convert_element_type.153, (f32[1,2048,8192]{2,1,0:T(8,128)}, f32[1,8192,2048]{2,1,0:T(8,128)}) %tuple.93, (pred[]{:T(512)}, s32[]{:T(128)}, bf16[1024,2048]{1,0:T(8,128)(2,1)}, ...), branch_computations={%region_3.3_spmd, %region_4.4_spmd.clone} | conditional | flops 172102778880 | bytes 557842560 | solution.py:87
  2203.3 159.6 %collective-permute-done.1 = bf16[1024,2048]{1,0:T(8,128)(2,1)} collective-permute-done((bf16[1024,2048]{1,0:T(8,128)(2,1)}, bf16[1024,2048]{1,0:T(8,128)(2,1)}, u32[]{:S(2)}, u32[]{:S(2)}) %collective-permute-start.1) | collective-permute-done | bytes 4194336 | tf_op jit(solution)/shard_map/while/body/eval_jaxpr/ppermute | solution.py:92
  2378.9 285.4 %conditional.7 = (bf16[1024,2048]{1,0:T(8,128)(2,1)}, f32[1,2048,8192]{2,1,0:T(8,128)}, f32[1,8192,2048]{2,1,0:T(8,128)}) conditional(s32[]{:T(128)} %convert_element_type.153, (f32[1,2048,8192]{2,1,0:T(8,128)}, f32[1,8192,2048]{2,1,0:T(8,128)}) %tuple.93, (pred[]{:T(512)}, s32[]{:T(128)}, bf16[1024,2048]{1,0:T(8,128)(2,1)}, ...), branch_computations={%region_3.3_spmd, %region_4.4_spmd.clone} | conditional | flops 172102778880 | bytes 557842560 | solution.py:87
  2681.5 71.9 %collective-permute-done.1 = bf16[1024,2048]{1,0:T(8,128)(2,1)} collective-permute-done((bf16[1024,2048]{1,0:T(8,128)(2,1)}, bf16[1024,2048]{1,0:T(8,128)(2,1)}, u32[]{:S(2)}, u32[]{:S(2)}) %collective-permute-start.1) | collective-permute-done | bytes 4194336 | tf_op jit(solution)/shard_map/while/body/eval_jaxpr/ppermute | solution.py:92
  2768.2 285.5 %conditional.7 = (bf16[1024,2048]{1,0:T(8,128)(2,1)}, f32[1,2048,8192]{2,1,0:T(8,128)}, f32[1,8192,2048]{2,1,0:T(8,128)}) conditional(s32[]{:T(128)} %convert_element_type.153, (f32[1,2048,8192]{2,1,0:T(8,128)}, f32[1,8192,2048]{2,1,0:T(8,128)}) %tuple.93, (pred[]{:T(512)}, s32[]{:T(128)}, bf16[1024,2048]{1,0:T(8,128)(2,1)}, ...), branch_computations={%region_3.3_spmd, %region_4.4_spmd.clone} | conditional | flops 172102778880 | bytes 557842560 | solution.py:87
  3072.2 69.6 %collective-permute-done.1 = bf16[1024,2048]{1,0:T(8,128)(2,1)} collective-permute-done((bf16[1024,2048]{1,0:T(8,128)(2,1)}, bf16[1024,2048]{1,0:T(8,128)(2,1)}, u32[]{:S(2)}, u32[]{:S(2)}) %collective-permute-start.1) | collective-permute-done | bytes 4194336 | tf_op jit(solution)/shard_map/while/body/eval_jaxpr/ppermute | solution.py:92
  3157.0 285.4 %conditional.7 = (bf16[1024,2048]{1,0:T(8,128)(2,1)}, f32[1,2048,8192]{2,1,0:T(8,128)}, f32[1,8192,2048]{2,1,0:T(8,128)}) conditional(s32[]{:T(128)} %convert_element_type.153, (f32[1,2048,8192]{2,1,0:T(8,128)}, f32[1,8192,2048]{2,1,0:T(8,128)}) %tuple.93, (pred[]{:T(512)}, s32[]{:T(128)}, bf16[1024,2048]{1,0:T(8,128)(2,1)}, ...), branch_computations={%region_3.3_spmd, %region_4.4_spmd.clone} | conditional | flops 172102778880 | bytes 557842560 | solution.py:87
  3550.9 284.7 %collective-permute-start.1 = (bf16[1024,2048]{1,0:T(8,128)(2,1)}, bf16[1024,2048]{1,0:T(8,128)(2,1)}, u32[]{:S(2)}, u32[]{:S(2)}) collective-permute-start(bf16[1024,2048]{1,0:T(8,128)(2,1)} %get-tuple-element.824), channel_id=1, source_target_pairs={{2,0},{4,2},{6,4},{3,1},{5,3},{7,5}} | collective-permute-start | bytes 12582920 | tf_op jit(solution)/shard_map/while/body/eval_jaxpr/ppermute | solution.py:92
  4002.5 78.0 %reduce-scatter.3.cloned.1.call-done = f32[1,1024,8192]{2,1,0:T(8,128)} async-done(((f32[1,2048,8192]{2,1,0:T(8,128)}), f32[1,1024,8192]{2,1,0:T(8,128)}) %reduce-scatter.3.cloned.1.call-update) | async-done | bytes 33554448 | tf_op jit(solution)/shard_map/reduce_scatter | solution.py:98
  (142 shorter events, 2417.3 us)
Async XLA Ops:
  7.2 3995.4 %reduce-scatter.5.cloned.1.call-start = ((), (), s32[]{:S(2)}) async-start(), calls=%async_computation.3 | async-start | bytes 100663296 | tf_op jit(solution)/shard_map/reduce_scatter | solution.py:99
  71.2 180.5 %collective-permute-start = (bf16[1024,2048]{1,0:T(8,128)(2,1)}, bf16[1024,2048]{1,0:T(8,128)(2,1)}, u32[]{:S(2)}, u32[]{:S(2)}) collective-permute-start(bf16[1024,2048]{1,0:T(8,128)(2,1)} %get-tuple-element.823), channel_id=1, source_target_pairs={{0,2},{2,4},{4,6},{1,3},{3,5},{5,7}} | collective-permute-start | bytes 12582920 | tf_op jit(solution)/shard_map/while/body/eval_jaxpr/ppermute | solution.py:91
  76.9 183.1 %collective-permute-start.1 = (bf16[1024,2048]{1,0:T(8,128)(2,1)}, bf16[1024,2048]{1,0:T(8,128)(2,1)}, u32[]{:S(2)}, u32[]{:S(2)}) collective-permute-start(bf16[1024,2048]{1,0:T(8,128)(2,1)} %get-tuple-element.824), channel_id=1, source_target_pairs={{2,0},{4,2},{6,4},{3,1},{5,3},{7,5}} | collective-permute-start | bytes 12582920 | tf_op jit(solution)/shard_map/while/body/eval_jaxpr/ppermute | solution.py:92
  360.2 93.6 %collective-permute-start = (bf16[1024,2048]{1,0:T(8,128)(2,1)}, bf16[1024,2048]{1,0:T(8,128)(2,1)}, u32[]{:S(2)}, u32[]{:S(2)}) collective-permute-start(bf16[1024,2048]{1,0:T(8,128)(2,1)} %get-tuple-element.823), channel_id=1, source_target_pairs={{0,2},{2,4},{4,6},{1,3},{3,5},{5,7}} | collective-permute-start | bytes 12582920 | tf_op jit(solution)/shard_map/while/body/eval_jaxpr/ppermute | solution.py:91
  364.7 177.0 %collective-permute-start.1 = (bf16[1024,2048]{1,0:T(8,128)(2,1)}, bf16[1024,2048]{1,0:T(8,128)(2,1)}, u32[]{:S(2)}, u32[]{:S(2)}) collective-permute-start(bf16[1024,2048]{1,0:T(8,128)(2,1)} %get-tuple-element.824), channel_id=1, source_target_pairs={{2,0},{4,2},{6,4},{3,1},{5,3},{7,5}} | collective-permute-start | bytes 12582920 | tf_op jit(solution)/shard_map/while/body/eval_jaxpr/ppermute | solution.py:92
  641.9 93.1 %collective-permute-start = (bf16[1024,2048]{1,0:T(8,128)(2,1)}, bf16[1024,2048]{1,0:T(8,128)(2,1)}, u32[]{:S(2)}, u32[]{:S(2)}) collective-permute-start(bf16[1024,2048]{1,0:T(8,128)(2,1)} %get-tuple-element.823), channel_id=1, source_target_pairs={{0,2},{2,4},{4,6},{1,3},{3,5},{5,7}} | collective-permute-start | bytes 12582920 | tf_op jit(solution)/shard_map/while/body/eval_jaxpr/ppermute | solution.py:91
  646.4 176.4 %collective-permute-start.1 = (bf16[1024,2048]{1,0:T(8,128)(2,1)}, bf16[1024,2048]{1,0:T(8,128)(2,1)}, u32[]{:S(2)}, u32[]{:S(2)}) collective-permute-start(bf16[1024,2048]{1,0:T(8,128)(2,1)} %get-tuple-element.824), channel_id=1, source_target_pairs={{2,0},{4,2},{6,4},{3,1},{5,3},{7,5}} | collective-permute-start | bytes 12582920 | tf_op jit(solution)/shard_map/while/body/eval_jaxpr/ppermute | solution.py:92
  923.0 92.5 %collective-permute-start = (bf16[1024,2048]{1,0:T(8,128)(2,1)}, bf16[1024,2048]{1,0:T(8,128)(2,1)}, u32[]{:S(2)}, u32[]{:S(2)}) collective-permute-start(bf16[1024,2048]{1,0:T(8,128)(2,1)} %get-tuple-element.823), channel_id=1, source_target_pairs={{0,2},{2,4},{4,6},{1,3},{3,5},{5,7}} | collective-permute-start | bytes 12582920 | tf_op jit(solution)/shard_map/while/body/eval_jaxpr/ppermute | solution.py:91
  927.5 175.8 %collective-permute-start.1 = (bf16[1024,2048]{1,0:T(8,128)(2,1)}, bf16[1024,2048]{1,0:T(8,128)(2,1)}, u32[]{:S(2)}, u32[]{:S(2)}) collective-permute-start(bf16[1024,2048]{1,0:T(8,128)(2,1)} %get-tuple-element.824), channel_id=1, source_target_pairs={{2,0},{4,2},{6,4},{3,1},{5,3},{7,5}} | collective-permute-start | bytes 12582920 | tf_op jit(solution)/shard_map/while/body/eval_jaxpr/ppermute | solution.py:92
  1203.5 91.9 %collective-permute-start = (bf16[1024,2048]{1,0:T(8,128)(2,1)}, bf16[1024,2048]{1,0:T(8,128)(2,1)}, u32[]{:S(2)}, u32[]{:S(2)}) collective-permute-start(bf16[1024,2048]{1,0:T(8,128)(2,1)} %get-tuple-element.823), channel_id=1, source_target_pairs={{0,2},{2,4},{4,6},{1,3},{3,5},{5,7}} | collective-permute-start | bytes 12582920 | tf_op jit(solution)/shard_map/while/body/eval_jaxpr/ppermute | solution.py:91
  1208.0 175.2 %collective-permute-start.1 = (bf16[1024,2048]{1,0:T(8,128)(2,1)}, bf16[1024,2048]{1,0:T(8,128)(2,1)}, u32[]{:S(2)}, u32[]{:S(2)}) collective-permute-start(bf16[1024,2048]{1,0:T(8,128)(2,1)} %get-tuple-element.824), channel_id=1, source_target_pairs={{2,0},{4,2},{6,4},{3,1},{5,3},{7,5}} | collective-permute-start | bytes 12582920 | tf_op jit(solution)/shard_map/while/body/eval_jaxpr/ppermute | solution.py:92
  1392.4 206.2 %collective-permute-start = (bf16[1024,2048]{1,0:T(8,128)(2,1)}, bf16[1024,2048]{1,0:T(8,128)(2,1)}, u32[]{:S(2)}, u32[]{:S(2)}) collective-permute-start(bf16[1024,2048]{1,0:T(8,128)(2,1)} %get-tuple-element.823), channel_id=1, source_target_pairs={{0,2},{2,4},{4,6},{1,3},{3,5},{5,7}} | collective-permute-start | bytes 12582920 | tf_op jit(solution)/shard_map/while/body/eval_jaxpr/ppermute | solution.py:91
  1514.7 371.8 %collective-permute-start.1 = (bf16[1024,2048]{1,0:T(8,128)(2,1)}, bf16[1024,2048]{1,0:T(8,128)(2,1)}, u32[]{:S(2)}, u32[]{:S(2)}) collective-permute-start(bf16[1024,2048]{1,0:T(8,128)(2,1)} %get-tuple-element.824), channel_id=1, source_target_pairs={{2,0},{4,2},{6,4},{3,1},{5,3},{7,5}} | collective-permute-start | bytes 12582920 | tf_op jit(solution)/shard_map/while/body/eval_jaxpr/ppermute | solution.py:92
  1895.7 307.5 %collective-permute-start = (bf16[1024,2048]{1,0:T(8,128)(2,1)}, bf16[1024,2048]{1,0:T(8,128)(2,1)}, u32[]{:S(2)}, u32[]{:S(2)}) collective-permute-start(bf16[1024,2048]{1,0:T(8,128)(2,1)} %get-tuple-element.823), channel_id=1, source_target_pairs={{0,2},{2,4},{4,6},{1,3},{3,5},{5,7}} | collective-permute-start | bytes 12582920 | tf_op jit(solution)/shard_map/while/body/eval_jaxpr/ppermute | solution.py:91
  2188.2 174.7 %collective-permute-start.1 = (bf16[1024,2048]{1,0:T(8,128)(2,1)}, bf16[1024,2048]{1,0:T(8,128)(2,1)}, u32[]{:S(2)}, u32[]{:S(2)}) collective-permute-start(bf16[1024,2048]{1,0:T(8,128)(2,1)} %get-tuple-element.824), channel_id=1, source_target_pairs={{2,0},{4,2},{6,4},{3,1},{5,3},{7,5}} | collective-permute-start | bytes 12582920 | tf_op jit(solution)/shard_map/while/body/eval_jaxpr/ppermute | solution.py:92
  2376.1 305.3 %collective-permute-start = (bf16[1024,2048]{1,0:T(8,128)(2,1)}, bf16[1024,2048]{1,0:T(8,128)(2,1)}, u32[]{:S(2)}, u32[]{:S(2)}) collective-permute-start(bf16[1024,2048]{1,0:T(8,128)(2,1)} %get-tuple-element.823), channel_id=1, source_target_pairs={{0,2},{2,4},{4,6},{1,3},{3,5},{5,7}} | collective-permute-start | bytes 12582920 | tf_op jit(solution)/shard_map/while/body/eval_jaxpr/ppermute | solution.py:91
  2664.3 89.0 %collective-permute-start.1 = (bf16[1024,2048]{1,0:T(8,128)(2,1)}, bf16[1024,2048]{1,0:T(8,128)(2,1)}, u32[]{:S(2)}, u32[]{:S(2)}) collective-permute-start(bf16[1024,2048]{1,0:T(8,128)(2,1)} %get-tuple-element.824), channel_id=1, source_target_pairs={{2,0},{4,2},{6,4},{3,1},{5,3},{7,5}} | collective-permute-start | bytes 12582920 | tf_op jit(solution)/shard_map/while/body/eval_jaxpr/ppermute | solution.py:92
  2766.2 305.9 %collective-permute-start = (bf16[1024,2048]{1,0:T(8,128)(2,1)}, bf16[1024,2048]{1,0:T(8,128)(2,1)}, u32[]{:S(2)}, u32[]{:S(2)}) collective-permute-start(bf16[1024,2048]{1,0:T(8,128)(2,1)} %get-tuple-element.823), channel_id=1, source_target_pairs={{0,2},{2,4},{4,6},{1,3},{3,5},{5,7}} | collective-permute-start | bytes 12582920 | tf_op jit(solution)/shard_map/while/body/eval_jaxpr/ppermute | solution.py:91
  3053.7 88.0 %collective-permute-start.1 = (bf16[1024,2048]{1,0:T(8,128)(2,1)}, bf16[1024,2048]{1,0:T(8,128)(2,1)}, u32[]{:S(2)}, u32[]{:S(2)}) collective-permute-start(bf16[1024,2048]{1,0:T(8,128)(2,1)} %get-tuple-element.824), channel_id=1, source_target_pairs={{2,0},{4,2},{6,4},{3,1},{5,3},{7,5}} | collective-permute-start | bytes 12582920 | tf_op jit(solution)/shard_map/while/body/eval_jaxpr/ppermute | solution.py:92
  3155.1 305.9 %collective-permute-start = (bf16[1024,2048]{1,0:T(8,128)(2,1)}, bf16[1024,2048]{1,0:T(8,128)(2,1)}, u32[]{:S(2)}, u32[]{:S(2)}) collective-permute-start(bf16[1024,2048]{1,0:T(8,128)(2,1)} %get-tuple-element.823), channel_id=1, source_target_pairs={{0,2},{2,4},{4,6},{1,3},{3,5},{5,7}} | collective-permute-start | bytes 12582920 | tf_op jit(solution)/shard_map/while/body/eval_jaxpr/ppermute | solution.py:91
  3442.4 87.1 %collective-permute-start.1 = (bf16[1024,2048]{1,0:T(8,128)(2,1)}, bf16[1024,2048]{1,0:T(8,128)(2,1)}, u32[]{:S(2)}, u32[]{:S(2)}) collective-permute-start(bf16[1024,2048]{1,0:T(8,128)(2,1)} %get-tuple-element.824), channel_id=1, source_target_pairs={{2,0},{4,2},{6,4},{3,1},{5,3},{7,5}} | collective-permute-start | bytes 12582920 | tf_op jit(solution)/shard_map/while/body/eval_jaxpr/ppermute | solution.py:92
  3542.4 306.4 %collective-permute-start = (bf16[1024,2048]{1,0:T(8,128)(2,1)}, bf16[1024,2048]{1,0:T(8,128)(2,1)}, u32[]{:S(2)}, u32[]{:S(2)}) collective-permute-start(bf16[1024,2048]{1,0:T(8,128)(2,1)} %get-tuple-element.823), channel_id=1, source_target_pairs={{0,2},{2,4},{4,6},{1,3},{3,5},{5,7}} | collective-permute-start | bytes 12582920 | tf_op jit(solution)/shard_map/while/body/eval_jaxpr/ppermute | solution.py:91
  3550.9 365.6 %collective-permute-start.1 = (bf16[1024,2048]{1,0:T(8,128)(2,1)}, bf16[1024,2048]{1,0:T(8,128)(2,1)}, u32[]{:S(2)}, u32[]{:S(2)}) collective-permute-start(bf16[1024,2048]{1,0:T(8,128)(2,1)} %get-tuple-element.824), channel_id=1, source_target_pairs={{2,0},{4,2},{6,4},{3,1},{5,3},{7,5}} | collective-permute-start | bytes 12582920 | tf_op jit(solution)/shard_map/while/body/eval_jaxpr/ppermute | solution.py:92
  3917.9 162.6 %reduce-scatter.3.cloned.1.call-start = ((), (), s32[]{:S(2)}) async-start(), calls=%async_computation.2 | async-start | bytes 100663296 | tf_op jit(solution)/shard_map/reduce_scatter | solution.py:98
Sparse Core Ops, SparseCore 0:
  3918.1 84.4 reduce-scatter.4
  4005.4 75.0 reduce-scatter.2
where the time goes:
time: 4090 us
  waiting for transfers between devices  1630 us (40%)
  matrix products  1490 us (36%)
  starting transfers between devices  563 us (14%)
  local copies, waits for them, and re-layouts  190 us (5%)
  other arithmetic  132 us (3%)
    ppermute x11, waiting for transfers between devices, tick(): recv_bwd = lax.ppermute(grad_out, 'stage', bwd_perm)  1080 us
    ppermute x11, starting transfers between devices, tick(): recv_bwd = lax.ppermute(grad_out, 'stage', bwd_perm)  417 us
    ppermute x11, waiting for transfers between devices, tick(): recv_fwd = lax.ppermute(h_out, 'stage', fwd_perm)  417 us
    dot_general x4, matrix products, layer_backward(): lax.dot_general(gelu_out, grad_out, CONTRACT_ROWS, preferred_element_type...  266 us
    dot_general x4, matrix products, layer_backward(): lax.dot_general(h_in, grad_pre, CONTRACT_ROWS, preferred_element_type=jnp...  252 us
    dot_general x4, matrix products, layer_backward(): lax.dot_general(grad_out, w_down, CONTRACT_COLS, preferred_element_type=j...  251 us
    dot_general x4, matrix products, layer_forward(): pre_act = jnp.dot(h_in, w_up, preferred_element_type=jnp.float32)  193 us
    dot_general x4, matrix products, layer_forward(): branch = jnp.dot(gelu_out, w_down, preferred_element_type=jnp.float32)  185 us
  transfers between devices with their start and end apart: 24, of which 19 were waited for; matrix products, arithmetic and copies ran while one was open for 32% of the time, Pallas kernels for 0%

commit v1 on v0

v1 whole, which is shorter than its diff:
```python
import jax
import jax.numpy as jnp
from jax import lax
from jax.sharding import PartitionSpec as P

CONTRACT_ROWS = (((0,), (0,)), ((), ()))
CONTRACT_COLS = (((1,), (1,)), ((), ()))
C0 = 0.7978845608028654
C1 = 0.044715
CHUNK = 512


def gelu_and_slope(u):
    u2 = u * u
    half = 0.5 * jnp.tanh(u * (C0 + (C0 * C1) * u2)) + 0.5
    g = u * half
    slope = half + (g * (1.0 - half)) * (2.0 * C0 + (6.0 * C0 * C1) * u2)
    return g.astype(jnp.bfloat16), slope


def solution(mesh):
    n_stage = mesh.shape['stage']
    n_data = mesh.shape['data']
    fwd_perm = [(k, k + 1) for k in range(n_stage - 1)]
    bwd_perm = [(k + 1, k) for k in range(n_stage - 1)]

    def per_device(inputs, targets, w_up, w_down):
        n_micro, n_tok, width = inputs.shape
        ffn = w_up.shape[2]
        rows = n_micro * n_tok
        n_chunk = rows // CHUNK
        x = inputs.reshape(rows, width)
        y = targets.reshape(rows, width)
        w1 = w_up[0]
        w2 = w_down[0]
        stage_id = lax.axis_index('stage')
        is_first = stage_id == 0
        is_last = stage_id == n_stage - 1
        inv_total = 1.0 / (n_data * rows)
        spare = rows

        def rows_of(a, at):
            return lax.dynamic_slice_in_dim(a, at, CHUNK, 0)

        def put(a, v, at):
            return lax.dynamic_update_slice_in_dim(a, v, at, 0)

        def tick(t, st):
            recv_f, recv_b, sh, sg, sd, sq, se, loss = st
            f = t - stage_id
            f_ok = (f >= 0) & (f < n_chunk)
            f_at = jnp.clip(f, 0, n_chunk - 1) * CHUNK
            f_to = jnp.where(f_ok, f_at, spare)
            h = jnp.where(is_first, rows_of(x, f_at), recv_f)
            g, d = gelu_and_slope(jnp.dot(h, w1, preferred_element_type=jnp.float32))
            sg = put(sg, g, f_to)
            sd = put(sd, d, f_to)
            sh = put(sh, h, f_to)
            v = jnp.dot(g, w2, preferred_element_type=jnp.float32)
            h_out = (h.astype(jnp.float32) + v).astype(jnp.bfloat16)
            send_f = lax.ppermute(h_out, 'stage', fwd_perm)
            diff = h_out.astype(jnp.float32) - rows_of(y, f_at).astype(jnp.float32)
            loss = loss + jnp.where(f_ok & is_last, jnp.sum(diff * diff), 0.0)
            top = (diff * inv_total).astype(jnp.bfloat16)

            b = t - (2 * (n_stage - 1) - stage_id)
            b_ok = (b >= 0) & (b < n_chunk)
            b_at = jnp.clip(b, 0, n_chunk - 1) * CHUNK
            b_to = jnp.where(b_ok, b_at, spare)
            e = jnp.where(is_last, top, recv_b)
            p = lax.dot_general(e, w2, CONTRACT_COLS, preferred_element_type=jnp.float32).astype(jnp.bfloat16)
            q = (p.astype(jnp.float32) * rows_of(sd, b_at)).astype(jnp.bfloat16)
            sq = put(sq, q, b_to)
            se = put(se, e, b_to)
            back = lax.dot_general(q, w1, CONTRACT_COLS, preferred_element_type=jnp.float32)
            e_out = (e.astype(jnp.float32) + back).astype(jnp.bfloat16)
            send_b = lax.ppermute(e_out, 'stage', bwd_perm)
            return send_f, send_b, sh, sg, sd, sq, se, loss

        def zeros(cols, dt=jnp.bfloat16):
            return jnp.zeros((rows + CHUNK, cols), dt)

        z = jnp.zeros((CHUNK, width), jnp.bfloat16)
        init = (z, z, zeros(width), zeros(ffn), zeros(ffn, jnp.float32), zeros(ffn), zeros(width), jnp.zeros((), jnp.float32))
        n_tick = n_chunk + 2 * (n_stage - 1)
        _, _, sh, sg, _, sq, se, loss = lax.fori_loop(0, n_tick, tick, init)
        half = width // n_data
        mine = lax.axis_index('data') * half
        other = (n_data - 1) * half - mine
        swap = [(0, 1), (1, 0)]
        sh, sg, sq, se = sh[:rows], sg[:rows], sq[:rows], se[:rows]

        def cols(a, at):
            return lax.dynamic_slice_in_dim(a, at, half, 1)

        def tn(a, b):
            return lax.dot_general(a, b, CONTRACT_ROWS, preferred_element_type=jnp.float32)

        up_other = lax.ppermute(tn(cols(sh, other), sq), 'data', swap)
        down_other = lax.ppermute(tn(sg, cols(se, other)), 'data', swap)
        g_up = tn(cols(sh, mine), sq) + up_other
        g_down = tn(sg, cols(se, mine)) + down_other
        loss_total = lax.psum(loss, ('stage', 'data')) * (0.5 * inv_total)
        return loss_total, g_up[None], g_down[None]

    return jax.shard_map(per_device, mesh=mesh, in_specs=(P('data', None, None), P('data', None, None), P('stage', None, None), P('stage', None, None)), out_specs=(P(), P('stage', 'data', None), P('stage', None, 'data')), check_vma=False)
```

time: 4090 us -> 3490 us (0.85)
  waiting for transfers between devices: 1630 us -> 895 us
  matrix products: 1490 us -> 1990 us
  starting transfers between devices: 563 us -> 108 us
  other arithmetic: 132 us -> 260 us
  local copies, waits for them, and re-layouts: 190 us -> 137 us
    ppermute x22 -> x30, waiting for transfers between devices: 1500 us -> 895 us  [the longest x14 575 us: tick(): send_f = lax.ppermute(h_out, 'stage', fwd_perm)]
    dot_general x28 -> x60, matrix products: 1490 us -> 1990 us  [the longest x14 485 us: tick(): v = jnp.dot(g, w2, preferred_element_type=jnp.float32)]
    ppermute x22 -> x30, starting transfers between devices: 563 us -> 108 us  [the longest x14 69.6 us: tick(): send_f = lax.ppermute(h_out, 'stage', fwd_perm)]
    dynamic_update_slice x0 -> x28, other arithmetic: none -> 204 us  [put(): return lax.dynamic_update_slice_in_dim(a, v, at, 0)]
    reduce_scatter x2 -> x0, waiting for transfers between devices: 128 us -> none  [the longest x1 78 us: per_device(): lax.psum_scatter(final_state[4], 'data', scatter_dimension=1, tiled=True)]
    dynamic_update_slice x11 -> x0, local copies, waits for them, and re-layouts: 52.7 us -> none  [tick(): stash = lax.dynamic_update_index_in_dim(stash, layer_ins, fwd_slot, 0)]
    reduce_sum x11 -> x14, other arithmetic: 84.7 us -> 55.8 us  [tick(): loss = loss + jnp.where(f_ok & is_last, jnp.sum(diff * diff), 0.0)]
  transfers between devices with their start and end apart: 24 -> 30, of which waited for: 19 -> 28; matrix products, arithmetic and copies ran while one was open for 32% -> 11% of each run, Pallas kernels for 0% -> 0%
where the time goes in v1:
time: 3490 us; the launch traced here: 3470 us
  matrix products  1990 us (57%)
  waiting for transfers between devices  895 us (26%)
  other arithmetic  260 us (7%)
  local copies, waits for them, and re-layouts  137 us (4%)
  starting transfers between devices  108 us (3%)
  blocking collectives  66.9 us (2%)
    ppermute x14, waiting for transfers between devices, tick(): send_f = lax.ppermute(h_out, 'stage', fwd_perm)  575 us
    dot_general x14, matrix products, tick(): v = jnp.dot(g, w2, preferred_element_type=jnp.float32)  485 us
    dot_general x14, matrix products, tick(): g, d = gelu_and_slope(jnp.dot(h, w1, preferred_element_type=jnp.float32))  452 us
    dot_general x14, matrix products, tick(): lax.dot_general(e, w2, CONTRACT_COLS, preferred_element_type=jnp.float32)  387 us
    dot_general x14, matrix products, tick(): lax.dot_general(q, w1, CONTRACT_COLS, preferred_element_type=jnp.float32)  346 us
    dot_general x4, matrix products, tn(): lax.dot_general(a, b, CONTRACT_ROWS, preferred_element_type=jnp.float32)  321 us
    ppermute x14, waiting for transfers between devices, tick(): send_b = lax.ppermute(e_out, 'stage', bwd_perm)  320 us
    dynamic_update_slice x28, other arithmetic, put(): return lax.dynamic_update_slice_in_dim(a, v, at, 0)  204 us
  transfers between devices with their start and end apart: 30, of which 28 were waited for; matrix products, arithmetic and copies ran while one was open for 11% of the time, Pallas kernels for 0%

profile of v1, /device:TPU:3, one launch (start us, length us, event | category | flops | bytes accessed | tf_op | source)
XLA Modules:
  0.0 3471.2 jit_solution(2579613954577414428)
XLA Ops:
  0.6 46.2 %broadcast_in_dim.13 = f32[4608,8192]{1,0:T(8,128)} broadcast(f32[]{:T(128)} %constant.137.clone.1), dimensions={} | broadcast | bytes 150994944 | tf_op jit(solution)/shard_map/broadcast_in_dim | solution.py:81
  109.0 2932.3 %while.28 = (s32[]{:T(128)}, bf16[512,2048]{1,0:T(8,128)(2,1)S(1)}, bf16[512,2048]{1,0:T(8,128)(2,1)}, bf16[4608,2048]{1,0:T(8,128)(2,1)}, bf16[4608,8192]{1,0:T...) while((s32[]{:T(128)}, bf16[512,2048]{1,0:T(8,128)(2,1)S(1)}, ...), condition=%wide.region_2.3_spmd, body=%wide.region_0.2_spmd.sunk | while | flops 68876763136 | bytes 310380160 | solution.py:86
  281.7 42.0 %collective-permute-done = bf16[512,2048]{1,0:T(8,128)(2,1)S(1)} collective-permute-done((bf16[512,2048]{1,0:T(8,128)(2,1)}, bf16[512,2048]{1,0:T(8,128)(2,1)S(1)}, u32[]{:S(2)}, u32[]{:S(2)}) %collective-permute-start) | collective-permute-done | bytes 2097184 | tf_op jit(solution)/shard_map/while/body/eval_jaxpr/ppermute | solution.py:61
  359.9 34.7 constant_dynamic-update-slice_fusion.9
  496.6 41.0 %collective-permute-done = bf16[512,2048]{1,0:T(8,128)(2,1)S(1)} collective-permute-done((bf16[512,2048]{1,0:T(8,128)(2,1)}, bf16[512,2048]{1,0:T(8,128)(2,1)S(1)}, u32[]{:S(2)}, u32[]{:S(2)}) %collective-permute-start) | collective-permute-done | bytes 2097184 | tf_op jit(solution)/shard_map/while/body/eval_jaxpr/ppermute | solution.py:61
  573.7 34.7 constant_dynamic-update-slice_fusion.9
  709.7 41.0 %collective-permute-done = bf16[512,2048]{1,0:T(8,128)(2,1)S(1)} collective-permute-done((bf16[512,2048]{1,0:T(8,128)(2,1)}, bf16[512,2048]{1,0:T(8,128)(2,1)S(1)}, u32[]{:S(2)}, u32[]{:S(2)}) %collective-permute-start) | collective-permute-done | bytes 2097184 | tf_op jit(solution)/shard_map/while/body/eval_jaxpr/ppermute | solution.py:61
  921.9 40.9 %collective-permute-done = bf16[512,2048]{1,0:T(8,128)(2,1)S(1)} collective-permute-done((bf16[512,2048]{1,0:T(8,128)(2,1)}, bf16[512,2048]{1,0:T(8,128)(2,1)S(1)}, u32[]{:S(2)}, u32[]{:S(2)}) %collective-permute-start) | collective-permute-done | bytes 2097184 | tf_op jit(solution)/shard_map/while/body/eval_jaxpr/ppermute | solution.py:61
  1133.3 41.0 %collective-permute-done = bf16[512,2048]{1,0:T(8,128)(2,1)S(1)} collective-permute-done((bf16[512,2048]{1,0:T(8,128)(2,1)}, bf16[512,2048]{1,0:T(8,128)(2,1)S(1)}, u32[]{:S(2)}, u32[]{:S(2)}) %collective-permute-start) | collective-permute-done | bytes 2097184 | tf_op jit(solution)/shard_map/while/body/eval_jaxpr/ppermute | solution.py:61
  1343.9 41.0 %collective-permute-done = bf16[512,2048]{1,0:T(8,128)(2,1)S(1)} collective-permute-done((bf16[512,2048]{1,0:T(8,128)(2,1)}, bf16[512,2048]{1,0:T(8,128)(2,1)S(1)}, u32[]{:S(2)}, u32[]{:S(2)}) %collective-permute-start) | collective-permute-done | bytes 2097184 | tf_op jit(solution)/shard_map/while/body/eval_jaxpr/ppermute | solution.py:61
  1553.7 40.9 %collective-permute-done = bf16[512,2048]{1,0:T(8,128)(2,1)S(1)} collective-permute-done((bf16[512,2048]{1,0:T(8,128)(2,1)}, bf16[512,2048]{1,0:T(8,128)(2,1)S(1)}, u32[]{:S(2)}, u32[]{:S(2)}) %collective-permute-start) | collective-permute-done | bytes 2097184 | tf_op jit(solution)/shard_map/while/body/eval_jaxpr/ppermute | solution.py:61
  1762.7 41.0 %collective-permute-done = bf16[512,2048]{1,0:T(8,128)(2,1)S(1)} collective-permute-done((bf16[512,2048]{1,0:T(8,128)(2,1)}, bf16[512,2048]{1,0:T(8,128)(2,1)S(1)}, u32[]{:S(2)}, u32[]{:S(2)}) %collective-permute-start) | collective-permute-done | bytes 2097184 | tf_op jit(solution)/shard_map/while/body/eval_jaxpr/ppermute | solution.py:61
  1971.0 40.9 %collective-permute-done = bf16[512,2048]{1,0:T(8,128)(2,1)S(1)} collective-permute-done((bf16[512,2048]{1,0:T(8,128)(2,1)}, bf16[512,2048]{1,0:T(8,128)(2,1)S(1)}, u32[]{:S(2)}, u32[]{:S(2)}) %collective-permute-start) | collective-permute-done | bytes 2097184 | tf_op jit(solution)/shard_map/while/body/eval_jaxpr/ppermute | solution.py:61
  2178.4 41.0 %collective-permute-done = bf16[512,2048]{1,0:T(8,128)(2,1)S(1)} collective-permute-done((bf16[512,2048]{1,0:T(8,128)(2,1)}, bf16[512,2048]{1,0:T(8,128)(2,1)S(1)}, u32[]{:S(2)}, u32[]{:S(2)}) %collective-permute-start) | collective-permute-done | bytes 2097184 | tf_op jit(solution)/shard_map/while/body/eval_jaxpr/ppermute | solution.py:61
  2385.1 40.9 %collective-permute-done = bf16[512,2048]{1,0:T(8,128)(2,1)S(1)} collective-permute-done((bf16[512,2048]{1,0:T(8,128)(2,1)}, bf16[512,2048]{1,0:T(8,128)(2,1)S(1)}, u32[]{:S(2)}, u32[]{:S(2)}) %collective-permute-start) | collective-permute-done | bytes 2097184 | tf_op jit(solution)/shard_map/while/body/eval_jaxpr/ppermute | solution.py:61
  2590.7 41.0 %collective-permute-done = bf16[512,2048]{1,0:T(8,128)(2,1)S(1)} collective-permute-done((bf16[512,2048]{1,0:T(8,128)(2,1)}, bf16[512,2048]{1,0:T(8,128)(2,1)S(1)}, u32[]{:S(2)}, u32[]{:S(2)}) %collective-permute-start) | collective-permute-done | bytes 2097184 | tf_op jit(solution)/shard_map/while/body/eval_jaxpr/ppermute | solution.py:61
  2667.9 34.7 constant_dynamic-update-slice_fusion.9
  2795.9 40.9 %collective-permute-done = bf16[512,2048]{1,0:T(8,128)(2,1)S(1)} collective-permute-done((bf16[512,2048]{1,0:T(8,128)(2,1)}, bf16[512,2048]{1,0:T(8,128)(2,1)S(1)}, u32[]{:S(2)}, u32[]{:S(2)}) %collective-permute-start) | collective-permute-done | bytes 2097184 | tf_op jit(solution)/shard_map/while/body/eval_jaxpr/ppermute | solution.py:61
  3000.0 41.0 %collective-permute-done = bf16[512,2048]{1,0:T(8,128)(2,1)S(1)} collective-permute-done((bf16[512,2048]{1,0:T(8,128)(2,1)}, bf16[512,2048]{1,0:T(8,128)(2,1)S(1)}, u32[]{:S(2)}, u32[]{:S(2)}) %collective-permute-start) | collective-permute-done | bytes 2097184 | tf_op jit(solution)/shard_map/while/body/eval_jaxpr/ppermute | solution.py:61
  3055.4 79.4 %fusion.4 = f32[8192,1024]{1,0:T(8,128)} fusion(bf16[4608,8192]{1,0:T(8,128)(2,1)} %get-tuple-element.338, bf16[4096,2048]{1,0:T(8,128)(2,1)} %slice.15, s32[]{:T(128)S(6)} %select_n.105), kind=kOutput, calls=%fused_computation.17 | convolution fusion | flops 68719476736 | bytes 109051904 | tf_op jit(solution)/shard_map/dot_general | solution.py:97
  3160.9 79.6 %fusion.8 = f32[1024,8192]{1,0:T(8,128)} fusion(bf16[4608,8192]{1,0:T(8,128)(2,1)} %get-tuple-element.337, bf16[4096,2048]{1,0:T(8,128)(2,1)} %slice.12, s32[]{:T(128)S(6)} %select_n.105), kind=kOutput, calls=%fused_computation.21 | convolution fusion | flops 68719476736 | bytes 109051904 | tf_op jit(solution)/shard_map/dot_general | solution.py:97
  3240.4 66.9 %psum.7 = f32[]{:T(128)} all-reduce(f32[]{:T(128)} %get-tuple-element.335), channel_id=1, replica_groups=mesh['stage'=4,'data'=2] {'stage','data'}, use_global_device_ids=true, to_apply=%region_3.4 | all-reduce | flops 1 | bytes 8 | tf_op jit(solution)/shard_map/psum | solution.py:103
  3308.0 80.7 %add_bitcast_fusion = f32[1,8192,1024]{2,1,0:T(8,128)} fusion(f32[8192,1024]{1,0:T(8,128)} %collective-permute-done.3, bf16[4608,8192]{1,0:T(8,128)(2,1)} %get-tuple-element.338, bf16[4096,2048]{1,0:T(8,128)(2,1)} %slice.15, s32[]{:T(128)S(6)} %select_n.104), kind=kOutput, calls=%fused_computation.25 | convolution fusion | flops 68727865344 | bytes 142606336 | tf_op jit(solution)/shard_map/dot_general | solution.py:97
  3388.6 80.9 %add_bitcast_fusion.1 = f32[1,1024,8192]{2,1,0:T(8,128)} fusion(f32[1024,8192]{1,0:T(8,128)} %collective-permute-done.2, bf16[4608,8192]{1,0:T(8,128)(2,1)} %get-tuple-element.337, bf16[4096,2048]{1,0:T(8,128)(2,1)} %slice.12, s32[]{:T(128)S(6)} %select_n.104), kind=kOutput, calls=%fused_computation.26 | convolution fusion | flops 68727865344 | bytes 142606336 | tf_op jit(solution)/shard_map/dot_general | solution.py:97
  (177 shorter events, 2345.8 us)
Async XLA Ops:
  232.3 49.4 %collective-permute-start.1 = (bf16[512,2048]{1,0:T(8,128)(2,1)}, bf16[512,2048]{1,0:T(8,128)(2,1)}, u32[]{:S(2)}, u32[]{:S(2)}) collective-permute-start(bf16[512,2048]{1,0:T(8,128)(2,1)} %add_convert_fusion.3), channel_id=1, source_target_pairs={{2,0},{4,2},{6,4},{3,1},{5,3},{7,5}} | collective-permute-start | bytes 6291464 | tf_op jit(solution)/shard_map/while/body/eval_jaxpr/ppermute | solution.py:77
  234.2 89.5 %collective-permute-start = (bf16[512,2048]{1,0:T(8,128)(2,1)}, bf16[512,2048]{1,0:T(8,128)(2,1)S(1)}, u32[]{:S(2)}, u32[]{:S(2)}) collective-permute-start(bf16[512,2048]{1,0:T(8,128)(2,1)} %get-tuple-element.497), channel_id=1, source_target_pairs={{0,2},{2,4},{4,6},{1,3},{3,5},{5,7}} | collective-permute-start | bytes 6291464 | tf_op jit(solution)/shard_map/while/body/eval_jaxpr/ppermute | solution.py:61
  446.9 49.6 %collective-permute-start.1 = (bf16[512,2048]{1,0:T(8,128)(2,1)}, bf16[512,2048]{1,0:T(8,128)(2,1)}, u32[]{:S(2)}, u32[]{:S(2)}) collective-permute-start(bf16[512,2048]{1,0:T(8,128)(2,1)} %add_convert_fusion.3), channel_id=1, source_target_pairs={{2,0},{4,2},{6,4},{3,1},{5,3},{7,5}} | collective-permute-start | bytes 6291464 | tf_op jit(solution)/shard_map/while/body/eval_jaxpr/ppermute | solution.py:77
  448.9 88.7 %collective-permute-start = (bf16[512,2048]{1,0:T(8,128)(2,1)}, bf16[512,2048]{1,0:T(8,128)(2,1)S(1)}, u32[]{:S(2)}, u32[]{:S(2)}) collective-permute-start(bf16[512,2048]{1,0:T(8,128)(2,1)} %get-tuple-element.497), channel_id=1, source_target_pairs={{0,2},{2,4},{4,6},{1,3},{3,5},{5,7}} | collective-permute-start | bytes 6291464 | tf_op jit(solution)/shard_map/while/body/eval_jaxpr/ppermute | solution.py:61
  660.8 48.9 %collective-permute-start.1 = (bf16[512,2048]{1,0:T(8,128)(2,1)}, bf16[512,2048]{1,0:T(8,128)(2,1)}, u32[]{:S(2)}, u32[]{:S(2)}) collective-permute-start(bf16[512,2048]{1,0:T(8,128)(2,1)} %add_convert_fusion.3), channel_id=1, source_target_pairs={{2,0},{4,2},{6,4},{3,1},{5,3},{7,5}} | collective-permute-start | bytes 6291464 | tf_op jit(solution)/shard_map/while/body/eval_jaxpr/ppermute | solution.py:77
  662.7 87.9 %collective-permute-start = (bf16[512,2048]{1,0:T(8,128)(2,1)}, bf16[512,2048]{1,0:T(8,128)(2,1)S(1)}, u32[]{:S(2)}, u32[]{:S(2)}) collective-permute-start(bf16[512,2048]{1,0:T(8,128)(2,1)} %get-tuple-element.497), channel_id=1, source_target_pairs={{0,2},{2,4},{4,6},{1,3},{3,5},{5,7}} | collective-permute-start | bytes 6291464 | tf_op jit(solution)/shard_map/while/body/eval_jaxpr/ppermute | solution.py:61
  873.8 48.1 %collective-permute-start.1 = (bf16[512,2048]{1,0:T(8,128)(2,1)}, bf16[512,2048]{1,0:T(8,128)(2,1)}, u32[]{:S(2)}, u32[]{:S(2)}) collective-permute-start(bf16[512,2048]{1,0:T(8,128)(2,1)} %add_convert_fusion.3), channel_id=1, source_target_pairs={{2,0},{4,2},{6,4},{3,1},{5,3},{7,5}} | collective-permute-start | bytes 6291464 | tf_op jit(solution)/shard_map/while/body/eval_jaxpr/ppermute | solution.py:77
  875.7 87.1 %collective-permute-start = (bf16[512,2048]{1,0:T(8,128)(2,1)}, bf16[512,2048]{1,0:T(8,128)(2,1)S(1)}, u32[]{:S(2)}, u32[]{:S(2)}) collective-permute-start(bf16[512,2048]{1,0:T(8,128)(2,1)} %get-tuple-element.497), channel_id=1, source_target_pairs={{0,2},{2,4},{4,6},{1,3},{3,5},{5,7}} | collective-permute-start | bytes 6291464 | tf_op jit(solution)/shard_map/while/body/eval_jaxpr/ppermute | solution.py:61
  1086.1 47.2 %collective-permute-start.1 = (bf16[512,2048]{1,0:T(8,128)(2,1)}, bf16[512,2048]{1,0:T(8,128)(2,1)}, u32[]{:S(2)}, u32[]{:S(2)}) collective-permute-start(bf16[512,2048]{1,0:T(8,128)(2,1)} %add_convert_fusion.3), channel_id=1, source_target_pairs={{2,0},{4,2},{6,4},{3,1},{5,3},{7,5}} | collective-permute-start | bytes 6291464 | tf_op jit(solution)/shard_map/while/body/eval_jaxpr/ppermute | solution.py:77
  1088.0 86.3 %collective-permute-start = (bf16[512,2048]{1,0:T(8,128)(2,1)}, bf16[512,2048]{1,0:T(8,128)(2,1)S(1)}, u32[]{:S(2)}, u32[]{:S(2)}) collective-permute-start(bf16[512,2048]{1,0:T(8,128)(2,1)} %get-tuple-element.497), channel_id=1, source_target_pairs={{0,2},{2,4},{4,6},{1,3},{3,5},{5,7}} | collective-permute-start | bytes 6291464 | tf_op jit(solution)/shard_map/while/body/eval_jaxpr/ppermute | solution.py:61
  1297.5 46.4 %collective-permute-start.1 = (bf16[512,2048]{1,0:T(8,128)(2,1)}, bf16[512,2048]{1,0:T(8,128)(2,1)}, u32[]{:S(2)}, u32[]{:S(2)}) collective-permute-start(bf16[512,2048]{1,0:T(8,128)(2,1)} %add_convert_fusion.3), channel_id=1, source_target_pairs={{2,0},{4,2},{6,4},{3,1},{5,3},{7,5}} | collective-permute-start | bytes 6291464 | tf_op jit(solution)/shard_map/while/body/eval_jaxpr/ppermute | solution.py:77
  1299.4 85.5 %collective-permute-start = (bf16[512,2048]{1,0:T(8,128)(2,1)}, bf16[512,2048]{1,0:T(8,128)(2,1)S(1)}, u32[]{:S(2)}, u32[]{:S(2)}) collective-permute-start(bf16[512,2048]{1,0:T(8,128)(2,1)} %get-tuple-element.497), channel_id=1, source_target_pairs={{0,2},{2,4},{4,6},{1,3},{3,5},{5,7}} | collective-permute-start | bytes 6291464 | tf_op jit(solution)/shard_map/while/body/eval_jaxpr/ppermute | solution.py:61
  1508.1 45.7 %collective-permute-start.1 = (bf16[512,2048]{1,0:T(8,128)(2,1)}, bf16[512,2048]{1,0:T(8,128)(2,1)}, u32[]{:S(2)}, u32[]{:S(2)}) collective-permute-start(bf16[512,2048]{1,0:T(8,128)(2,1)} %add_convert_fusion.3), channel_id=1, source_target_pairs={{2,0},{4,2},{6,4},{3,1},{5,3},{7,5}} | collective-permute-start | bytes 6291464 | tf_op jit(solution)/shard_map/while/body/eval_jaxpr/ppermute | solution.py:77
  1510.0 84.7 %collective-permute-start = (bf16[512,2048]{1,0:T(8,128)(2,1)}, bf16[512,2048]{1,0:T(8,128)(2,1)S(1)}, u32[]{:S(2)}, u32[]{:S(2)}) collective-permute-start(bf16[512,2048]{1,0:T(8,128)(2,1)} %get-tuple-element.497), channel_id=1, source_target_pairs={{0,2},{2,4},{4,6},{1,3},{3,5},{5,7}} | collective-permute-start | bytes 6291464 | tf_op jit(solution)/shard_map/while/body/eval_jaxpr/ppermute | solution.py:61
  1717.9 44.8 %collective-permute-start.1 = (bf16[512,2048]{1,0:T(8,128)(2,1)}, bf16[512,2048]{1,0:T(8,128)(2,1)}, u32[]{:S(2)}, u32[]{:S(2)}) collective-permute-start(bf16[512,2048]{1,0:T(8,128)(2,1)} %add_convert_fusion.3), channel_id=1, source_target_pairs={{2,0},{4,2},{6,4},{3,1},{5,3},{7,5}} | collective-permute-start | bytes 6291464 | tf_op jit(solution)/shard_map/while/body/eval_jaxpr/ppermute | solution.py:77
  1719.8 83.9 %collective-permute-start = (bf16[512,2048]{1,0:T(8,128)(2,1)}, bf16[512,2048]{1,0:T(8,128)(2,1)S(1)}, u32[]{:S(2)}, u32[]{:S(2)}) collective-permute-start(bf16[512,2048]{1,0:T(8,128)(2,1)} %get-tuple-element.497), channel_id=1, source_target_pairs={{0,2},{2,4},{4,6},{1,3},{3,5},{5,7}} | collective-permute-start | bytes 6291464 | tf_op jit(solution)/shard_map/while/body/eval_jaxpr/ppermute | solution.py:61
  1928.8 83.1 %collective-permute-start = (bf16[512,2048]{1,0:T(8,128)(2,1)}, bf16[512,2048]{1,0:T(8,128)(2,1)S(1)}, u32[]{:S(2)}, u32[]{:S(2)}) collective-permute-start(bf16[512,2048]{1,0:T(8,128)(2,1)} %get-tuple-element.497), channel_id=1, source_target_pairs={{0,2},{2,4},{4,6},{1,3},{3,5},{5,7}} | collective-permute-start | bytes 6291464 | tf_op jit(solution)/shard_map/while/body/eval_jaxpr/ppermute | solution.py:61
  2137.1 82.3 %collective-permute-start = (bf16[512,2048]{1,0:T(8,128)(2,1)}, bf16[512,2048]{1,0:T(8,128)(2,1)S(1)}, u32[]{:S(2)}, u32[]{:S(2)}) collective-permute-start(bf16[512,2048]{1,0:T(8,128)(2,1)} %get-tuple-element.497), channel_id=1, source_target_pairs={{0,2},{2,4},{4,6},{1,3},{3,5},{5,7}} | collective-permute-start | bytes 6291464 | tf_op jit(solution)/shard_map/while/body/eval_jaxpr/ppermute | solution.py:61
  2344.4 81.5 %collective-permute-start = (bf16[512,2048]{1,0:T(8,128)(2,1)}, bf16[512,2048]{1,0:T(8,128)(2,1)S(1)}, u32[]{:S(2)}, u32[]{:S(2)}) collective-permute-start(bf16[512,2048]{1,0:T(8,128)(2,1)} %get-tuple-element.497), channel_id=1, source_target_pairs={{0,2},{2,4},{4,6},{1,3},{3,5},{5,7}} | collective-permute-start | bytes 6291464 | tf_op jit(solution)/shard_map/while/body/eval_jaxpr/ppermute | solution.py:61
  2551.1 80.7 %collective-permute-start = (bf16[512,2048]{1,0:T(8,128)(2,1)}, bf16[512,2048]{1,0:T(8,128)(2,1)S(1)}, u32[]{:S(2)}, u32[]{:S(2)}) collective-permute-start(bf16[512,2048]{1,0:T(8,128)(2,1)} %get-tuple-element.497), channel_id=1, source_target_pairs={{0,2},{2,4},{4,6},{1,3},{3,5},{5,7}} | collective-permute-start | bytes 6291464 | tf_op jit(solution)/shard_map/while/body/eval_jaxpr/ppermute | solution.py:61
  2756.9 79.9 %collective-permute-start = (bf16[512,2048]{1,0:T(8,128)(2,1)}, bf16[512,2048]{1,0:T(8,128)(2,1)S(1)}, u32[]{:S(2)}, u32[]{:S(2)}) collective-permute-start(bf16[512,2048]{1,0:T(8,128)(2,1)} %get-tuple-element.497), channel_id=1, source_target_pairs={{0,2},{2,4},{4,6},{1,3},{3,5},{5,7}} | collective-permute-start | bytes 6291464 | tf_op jit(solution)/shard_map/while/body/eval_jaxpr/ppermute | solution.py:61
  2961.9 79.1 %collective-permute-start = (bf16[512,2048]{1,0:T(8,128)(2,1)}, bf16[512,2048]{1,0:T(8,128)(2,1)S(1)}, u32[]{:S(2)}, u32[]{:S(2)}) collective-permute-start(bf16[512,2048]{1,0:T(8,128)(2,1)} %get-tuple-element.497), channel_id=1, source_target_pairs={{0,2},{2,4},{4,6},{1,3},{3,5},{5,7}} | collective-permute-start | bytes 6291464 | tf_op jit(solution)/shard_map/while/body/eval_jaxpr/ppermute | solution.py:61
  3134.9 173.1 %collective-permute-start.3 = (f32[8192,1024]{1,0:T(8,128)}, f32[8192,1024]{1,0:T(8,128)}, u32[]{:S(2)}, u32[]{:S(2)}) collective-permute-start(f32[8192,1024]{1,0:T(8,128)} %fusion.4), channel_id=1, source_target_pairs={{0,1},{1,0},{2,3},{3,2},{4,5},{5,4},{6,7},{7,6}} | collective-permute-start | bytes 100663304 | tf_op jit(solution)/shard_map/ppermute | solution.py:100
  3240.4 148.2 %collective-permute-start.2 = (f32[1024,8192]{1,0:T(8,128)}, f32[1024,8192]{1,0:T(8,128)}, u32[]{:S(2)}, u32[]{:S(2)}) collective-permute-start(f32[1024,8192]{1,0:T(8,128)} %fusion.8), channel_id=1, source_target_pairs={{0,1},{1,0},{2,3},{3,2},{4,5},{5,4},{6,7},{7,6}} | collective-permute-start | bytes 100663304 | tf_op jit(solution)/shard_map/ppermute | solution.py:99
  (20 other events, 704.8 us)

commit v2 on v1

v2 whole, which is shorter than its diff:
```python
import functools

import jax
import jax.numpy as jnp
from jax import lax
from jax.experimental import pallas as pl
from jax.experimental.pallas import tpu as pltpu
from jax.sharding import PartitionSpec as P

BF16 = jnp.bfloat16
F32 = jnp.float32
C0 = 0.7978845608028654
C1 = 0.044715
ROWS = 256
CT = 1024
DT = 512
NSTEP = 4
RING = 4
NN = (((1,), (0,)), ((), ()))
NT = (((1,), (1,)), ((), ()))
TN = (((0,), (0,)), ((), ()))


def dot(a, b, dims):
    return lax.dot_general(a, b, dims, preferred_element_type=F32)


def pipeline_kernel(n_stage, n_data, n_chunk, inv_total,
                    x, y, w1, w2,
                    hs, gs, ds, qs, es, loss_out,
                    w1r, w2r, ring, gq, dbuf, inb, out, loss_acc, lbuf,
                    w1_sem, w2_sem, ring_sem, d_sem, gq_sem, in_sem, o_send,
                    h_recv, e_recv, y_sem, st_sem, l_send, l_recv):
    s = lax.axis_index('stage')
    peer = n_data - 1 - lax.axis_index('data')
    first = s == 0
    last = s == n_stage - 1
    half = w1r.shape[1]
    n_slot = 2 * n_chunk
    warm = n_chunk - 5 * s

    def order(k):
        j = jnp.maximum(k - warm, 0)
        left = n_chunk - warm
        early = k < warm
        mixed = j < 2 * left
        odd = lax.rem(j, 2) == 1
        is_f = early | (mixed & odd)
        idx = jnp.where(early, k, jnp.where(mixed, jnp.where(odd, warm + j // 2, j // 2), j - left))
        return is_f, idx

    def rows(i):
        return pl.ds(pl.multiple_of(i * ROWS, ROWS), ROWS)

    def cols(j, size, base=0):
        if isinstance(j, int):
            return pl.ds(base + j * size, size)
        return pl.ds(pl.multiple_of(base + j * size, size), size)

    def copy(src, dst, sem):
        return pltpu.make_async_copy(src, dst, sem)

    def start_f1(j):
        copy(w1.at[0, :, cols(j, CT, half)], ring.at[j], ring_sem.at[j]).start()

    def start_f2(j):
        for i in range(2):
            copy(w2.at[0, pl.ds(half + i * 2048, 2048), cols(j, DT)], ring.at[j, :, pl.ds(i * DT, DT)], ring_sem.at[j]).start()

    def start_b1(j):
        for i in range(2):
            copy(w2.at[0, cols(j, CT, half), pl.ds(i * CT, CT)], ring.at[j, pl.ds(i * CT, CT)], ring_sem.at[j]).start()

    def start_b2(j):
        for i in range(4):
            copy(w1.at[0, cols(j, DT), pl.ds(half + i * CT, CT)], ring.at[j, pl.ds(i * DT, DT)], ring_sem.at[j]).start()

    def start_slot(k, j):
        is_f, _ = order(k)

        @pl.when((k < n_slot) & is_f)
        def _():
            start_f1(j)

        @pl.when((k < n_slot) & jnp.logical_not(is_f))
        def _():
            start_b1(j)

    def wait_ring(r):
        copy(ring.at[r], ring.at[r], ring_sem.at[r]).wait()

    def d_cols(j, b):
        return cols(j, CT, b * half)

    def d_out_slot(j, b):
        return 2 + lax.rem(j, 3) if b else lax.rem(j, 2)

    def d_in_slot(j, b):
        return 3 * b + lax.rem(j, 2)

    def start_d_in(i, j):
        for b in range(2):
            copy(ds.at[rows(i), d_cols(j, b)], dbuf.at[d_in_slot(j, b)], d_sem.at[d_in_slot(j, b)]).start()

    def start_d_out(i, j, b):
        copy(dbuf.at[d_out_slot(j, b)], ds.at[rows(i), d_cols(j, b)], d_sem.at[d_out_slot(j, b)]).start()

    def wait_d(q):
        copy(dbuf.at[q], dbuf.at[q], d_sem.at[q]).wait()

    def needs_copy(k):
        is_f, _ = order(k)
        return is_f | jnp.logical_not(last)

    def ahead(k):
        return (first | (k >= warm)) & (k < n_slot)

    def load_in(k):
        is_f, i = order(k)
        b = lax.rem(k, 2)

        @pl.when(is_f & first)
        def _():
            copy(x.at[rows(i)], inb.at[b], in_sem.at[b]).start()

        @pl.when(is_f & jnp.logical_not(first))
        def _():
            copy(hs.at[rows(i)], hs.at[rows(i)], h_recv.at[i]).wait()
            copy(hs.at[rows(i)], inb.at[b], in_sem.at[b]).start()

        @pl.when(jnp.logical_not(is_f) & jnp.logical_not(last))
        def _():
            copy(es.at[rows(i)], es.at[rows(i)], e_recv.at[i]).wait()
            copy(es.at[rows(i)], inb.at[b], in_sem.at[b]).start()

    def before_next(k):
        is_f, i = order(k + 1)

        @pl.when(ahead(k + 1))
        def _():
            load_in(k + 1)

        @pl.when((k + 1 < n_slot) & jnp.logical_not(is_f))
        def _():
            start_d_in(i, 0)

    def next_stage(k, i, j):
        o = lax.rem(k, 2)
        return pltpu.make_async_remote_copy(
            src_ref=out.at[o, :, cols(j, DT)], dst_ref=hs.at[rows(i), cols(j, DT)],
            send_sem=o_send.at[o], recv_sem=h_recv.at[i],
            device_id={'stage': s + 1}, device_id_type=pl.DeviceIdType.MESH)

    def prev_stage(k, i, j):
        o = lax.rem(k, 2)
        return pltpu.make_async_remote_copy(
            src_ref=out.at[o, :, cols(j, DT)], dst_ref=es.at[rows(i), cols(j, DT)],
            send_sem=o_send.at[o], recv_sem=e_recv.at[i],
            device_id={'stage': s - 1}, device_id_type=pl.DeviceIdType.MESH)

    def sent(k):
        is_f, _ = order(k)
        return (is_f & jnp.logical_not(last)) | (jnp.logical_not(is_f) & jnp.logical_not(first))

    def wait_sent(k):
        @pl.when((k >= 0) & sent(jnp.maximum(k, 0)))
        def _():
            o = lax.rem(k, 2)
            copy(out.at[o], out.at[o], o_send.at[o]).wait()

    def gelu_tile(q, c):
        for r in range(0, ROWS, 16):
            for z in range(0, CT, 256):
                u = dbuf[q, pl.ds(r, 16), pl.ds(z, 256)]
                u2 = u * u
                h = 0.5 * jnp.tanh(u * (C0 + (C0 * C1) * u2)) + 0.5
                g = u * h
                gq[pl.ds(r, 16), pl.ds(pl.multiple_of(c + z, 256), 256)] = g.astype(BF16)
                dbuf[q, pl.ds(r, 16), pl.ds(z, 256)] = h + (g * (1.0 - h)) * (2.0 * C0 + (6.0 * C0 * C1) * u2)

    def g_out(i, j, b):
        copy(gq.at[:, d_cols(j, b)], gs.at[rows(i), d_cols(j, b)], gq_sem).start()

    def forward(k, i):
        p = lax.rem(k, 2)
        o = lax.rem(k, 2)

        def step1(j, carry):
            @pl.when(j == 0)
            def _():
                start_f1(2)
                start_f1(3)

            @pl.when(j >= 1)
            def _():
                start_f2(j - 1)

            @pl.when(j >= 2)
            def _():
                wait_d(lax.rem(j, 2))

            @pl.when(j >= 3)
            def _():
                wait_d(2)

            @pl.when(k == 0)
            def _():
                copy(w1r.at[:, cols(j, CT)], w1r.at[:, cols(j, CT)], w1_sem.at[j]).wait()

            wait_ring(j)
            jp = jnp.maximum(j - 1, 0)
            dbuf[d_out_slot(j, 0)] = dot(inb[p], w1r[:, cols(j, CT)], NN)
            gelu_tile(2 + lax.rem(j + 2, 3), half + jp * CT)
            dbuf[d_out_slot(j, 1)] = dot(inb[p], ring[j], NN)
            gelu_tile(d_out_slot(j, 0), j * CT)

            @pl.when(j >= 1)
            def _():
                g_out(i, j - 1, 1)
                start_d_out(i, j - 1, 1)

            g_out(i, j, 0)
            start_d_out(i, j, 0)
            return carry

        lax.fori_loop(0, NSTEP, step1, 0)

        @pl.when(last)
        def _():
            copy(inb.at[1 - p], inb.at[1 - p], y_sem).wait()

        wait_sent(k - 2)
        for jj in range(2):
            if jj == 0:
                start_f2(3)
                wait_d(3)
            else:
                start_slot(k + 1, 0)
                start_slot(k + 1, 1)
                for q in (0, 1, 4):
                    wait_d(q)
                before_next(k)

            @pl.when(k == 0)
            def _():
                for j in (2 * jj, 2 * jj + 1):
                    copy(w2r.at[:, cols(j, DT)], w2r.at[:, cols(j, DT)], w2_sem.at[j]).wait()

            for j in (2 * jj, 2 * jj + 1):
                wait_ring(j)
            for j in (2 * jj, 2 * jj + 1):
                v = dot(gq[:, pl.ds(0, half)], w2r[:, cols(j, DT)], NN)
                if j == 0:
                    dbuf[3, :, pl.ds(0, DT)] = v
                    gelu_tile(2, half + 3 * CT)
                    v = dbuf[3, :, pl.ds(0, DT)]
                v = v + dot(gq[:, pl.ds(half, 2048)], ring[j, :, pl.ds(0, DT)], NN)
                v = v + dot(gq[:, pl.ds(half + 2048, 2048)], ring[j, :, pl.ds(DT, DT)], NN)
                out[o, :, cols(j, DT)] = (inb[p, :, cols(j, DT)].astype(F32) + v).astype(BF16)
            if jj == 0:
                g_out(i, 3, 1)
                start_d_out(i, 3, 1)

            @pl.when(jnp.logical_not(last))
            def _():
                for j in (2 * jj, 2 * jj + 1):
                    next_stage(k, i, j).start()

            @pl.when(last)
            def _():
                for j in (2 * jj, 2 * jj + 1):
                    for r in range(0, ROWS, 16):
                        diff = out[o, pl.ds(r, 16), cols(j, DT)].astype(F32) - inb[1 - p, pl.ds(r, 16), cols(j, DT)].astype(F32)
                        loss_acc[...] += diff * diff
                        inb[1 - p, pl.ds(r, 16), cols(j, DT)] = (diff * inv_total).astype(BF16)

        wait_d(2)

    def backward(k, i):
        p = lax.rem(k, 2)
        o = lax.rem(k, 2)

        def step1(j, carry):
            @pl.when(j == 0)
            def _():
                start_b1(2)
                start_b1(3)

            @pl.when((j >= 1) & jnp.logical_not(first))
            def _():
                start_b2(j - 1)

            @pl.when((j >= 1) & (j < 3) & first)
            def _():
                start_slot(k + 1, j - 1)

            @pl.when(j < NSTEP - 1)
            def _():
                start_d_in(i, j + 1)

            @pl.when((j == NSTEP - 1) & first)
            def _():
                before_next(k)

            wait_d(d_in_slot(j, 0))
            wait_d(d_in_slot(j, 1))
            wait_ring(j)
            pa = dot(inb[p], w2r[cols(j, CT), :], NT).astype(BF16).astype(F32)
            gq[:, d_cols(j, 0)] = (pa * dbuf[d_in_slot(j, 0)]).astype(BF16)
            pb = dot(inb[p, :, pl.ds(0, CT)], ring[j, pl.ds(0, CT)], NT)
            pb = pb + dot(inb[p, :, pl.ds(CT, CT)], ring[j, pl.ds(CT, CT)], NT)
            pb = pb.astype(BF16).astype(F32)
            gq[:, d_cols(j, 1)] = (pb * dbuf[d_in_slot(j, 1)]).astype(BF16)
            for b in range(2):
                copy(gq.at[:, d_cols(j, b)], qs.at[rows(i), d_cols(j, b)], gq_sem).start()
            return carry

        lax.fori_loop(0, NSTEP, step1, 0)
        wait_sent(k - 2)

        @pl.when(jnp.logical_not(first))
        def _():
            def step2(jj, carry):
                @pl.when(jj == 0)
                def _():
                    start_b2(3)

                @pl.when(jj == 1)
                def _():
                    start_slot(k + 1, 0)
                    start_slot(k + 1, 1)
                    before_next(k)

                for z in range(2):
                    wait_ring(2 * jj + z)
                for z in range(2):
                    j = 2 * jj + z
                    v = dot(gq[:, pl.ds(0, half)], w1r[cols(j, DT), :], NT)
                    for c in range(4):
                        v = v + dot(gq[:, pl.ds(half + c * CT, CT)], ring[j, pl.ds(c * DT, DT)], NT)
                    out[o, :, cols(j, DT)] = (inb[p, :, cols(j, DT)].astype(F32) + v).astype(BF16)
                for z in range(2):
                    prev_stage(k, i, 2 * jj + z).start()
                return carry

            lax.fori_loop(0, 2, step2, 0)

    barrier = pltpu.get_barrier_semaphore()

    def hello(**to):
        pl.semaphore_signal(barrier, inc=1, device_id=to, device_id_type=pl.DeviceIdType.MESH)

    @pl.when(jnp.logical_not(first))
    def _():
        hello(stage=s - 1)

    @pl.when(jnp.logical_not(last))
    def _():
        hello(stage=s + 1)

    @pl.when(last)
    def _():
        hello(data=peer)

    @pl.when(first)
    def _():
        load_in(0)

    start_f1(0)
    for j in range(NSTEP):
        copy(w1.at[0, :, pl.ds(j * CT, CT)], w1r.at[:, pl.ds(j * CT, CT)], w1_sem.at[j]).start()
        if j == 0:
            start_f1(1)
    for j in range(NSTEP):
        copy(w2.at[0, pl.ds(0, half), pl.ds(j * DT, DT)], w2r.at[:, pl.ds(j * DT, DT)], w2_sem.at[j]).start()
    loss_acc[...] = jnp.zeros_like(loss_acc)

    @pl.when(first)
    def _():
        pl.semaphore_wait(barrier, 1)

    @pl.when(jnp.logical_not(first))
    def _():
        pl.semaphore_wait(barrier, 2)

    def slot(k, carry):
        is_f, i = order(k)
        p = lax.rem(k, 2)

        @pl.when(k > 0)
        def _():
            copy(gq, gq, gq_sem).wait()

        @pl.when(jnp.logical_not(ahead(k)))
        def _():
            load_in(k)

        @pl.when(needs_copy(k))
        def _():
            copy(inb.at[p], inb.at[p], in_sem.at[p]).wait()

        @pl.when(is_f & first)
        def _():
            copy(inb.at[p], hs.at[rows(i)], st_sem).start()

        @pl.when(jnp.logical_not(is_f) & last)
        def _():
            copy(inb.at[p], es.at[rows(i)], st_sem).start()

        @pl.when(is_f & last)
        def _():
            copy(y.at[rows(i)], inb.at[1 - p], y_sem).start()

        @pl.when(is_f)
        def _():
            forward(k, i)

        @pl.when(jnp.logical_not(is_f))
        def _():
            backward(k, i)

        @pl.when((is_f & first) | (jnp.logical_not(is_f) & last))
        def _():
            copy(inb.at[p], inb.at[p], st_sem).wait()

        return carry

    lax.fori_loop(0, n_slot, slot, 0)
    copy(gq, gq, gq_sem).wait()
    for k in range(n_slot - 2, n_slot):
        wait_sent(jnp.int32(k))

    def to_peer():
        return pltpu.make_async_remote_copy(
            src_ref=lbuf.at[0], dst_ref=lbuf.at[1], send_sem=l_send.at[0], recv_sem=l_recv.at[0],
            device_id={'data': peer}, device_id_type=pl.DeviceIdType.MESH)

    def to_prev():
        return pltpu.make_async_remote_copy(
            src_ref=lbuf.at[2], dst_ref=lbuf.at[2], send_sem=l_send.at[1], recv_sem=l_recv.at[1],
            device_id={'stage': s - 1}, device_id_type=pl.DeviceIdType.MESH)

    @pl.when(last)
    def _():
        lbuf[0] = loss_acc[pl.ds(0, 8), :] + loss_acc[pl.ds(8, 8), :]
        rdma = to_peer()
        rdma.start()
        rdma.wait()
        lbuf[2] = lbuf[0] + lbuf[1]

    @pl.when(jnp.logical_not(last))
    def _():
        copy(lbuf.at[2], lbuf.at[2], l_recv.at[1]).wait()

    loss_out[...] = lbuf[2]

    @pl.when(jnp.logical_not(first))
    def _():
        to_prev().start()
        copy(lbuf.at[2], lbuf.at[2], l_send.at[1]).wait()


def run_pipeline(n_stage, n_data, x, y, w1, w2):
    n_row, width = x.shape
    ffn = w1.shape[2]
    n_chunk = n_row // ROWS
    half = ffn // 2
    hbm = pl.BlockSpec(memory_space=pl.ANY)
    out = jax.ShapeDtypeStruct
    dma = pltpu.SemaphoreType.DMA
    flops = 8 * n_row * width * ffn
    return pl.pallas_call(
        functools.partial(pipeline_kernel, n_stage, n_data, n_chunk, 1.0 / (n_data * n_row)),
        out_shape=(out((n_row, width), BF16), out((n_row, ffn), BF16), out((n_row, ffn), F32),
                   out((n_row, ffn), BF16), out((n_row, width), BF16), out((8, DT), F32)),
        in_specs=[hbm] * 4,
        out_specs=(hbm,) * 5 + (pl.BlockSpec(memory_space=pltpu.VMEM),),
        scratch_shapes=[
            pltpu.VMEM((width, half), BF16), pltpu.VMEM((half, width), BF16),
            pltpu.VMEM((RING, width, CT), BF16), pltpu.VMEM((ROWS, ffn), BF16),
            pltpu.VMEM((5, ROWS, CT), F32), pltpu.VMEM((2, ROWS, width), BF16),
            pltpu.VMEM((2, ROWS, width), BF16), pltpu.VMEM((16, DT), F32),
            pltpu.VMEM((3, 8, DT), F32),
            dma((NSTEP,)), dma((NSTEP,)), dma((RING,)), dma((5,)), dma, dma((2,)), dma((2,)),
            dma((n_chunk,)), dma((n_chunk,)), dma, dma, dma((2,)), dma((2,)),
        ],
        compiler_params=pltpu.CompilerParams(collective_id=0, has_side_effects=True, vmem_limit_bytes=67043328),
        cost_estimate=pl.CostEstimate(flops=flops, bytes_accessed=1 << 30, transcendentals=n_row * ffn),
        name='pipeline',
    )(x, y, w1, w2)


def solution(mesh):
    n_stage = mesh.shape['stage']
    n_data = mesh.shape['data']

    def per_device(inputs, targets, w_up, w_down):
        n_micro, n_tok, width = inputs.shape
        n_row = n_micro * n_tok
        x = inputs.reshape(n_row, width)
        y = targets.reshape(n_row, width)
        hs, gs, _, qs, es, loss = run_pipeline(n_stage, n_data, x, y, w_up, w_down)
        half = width // n_data
        mine = lax.axis_index('data') * half
        other = (n_data - 1) * half - mine
        swap = [(0, 1), (1, 0)]

        def part(a, at):
            return lax.dynamic_slice_in_dim(a, at, half, 1)

        up_other = lax.ppermute(dot(part(hs, other), qs, TN), 'data', swap)
        down_other = lax.ppermute(dot(gs, part(es, other), TN), 'data', swap)
        g_up = dot(part(hs, mine), qs, TN) + up_other
        g_down = dot(gs, part(es, mine), TN) + down_other
        loss_total = jnp.sum(loss) * (0.5 / (n_data * n_row))
        return loss_total, g_up[None], g_down[None]

    return jax.shard_map(per_device, mesh=mesh, in_specs=(P('data', None, None), P('data', None, None), P('stage', None, None), P('stage', None, None)), out_specs=(P(), P('stage', 'data', None), P('stage', None, 'data')), check_vma=False)
```

time: 3490 us -> 1290 us (0.37)
  the two profiles are of different devices: /device:TPU:3 before, /device:TPU:0 now
where the time goes in v2:
time: 1290 us; the launch traced here: 1280 us
  Pallas kernels  956 us (74%)
  matrix products  321 us (25%)
    pallas_call x1, Pallas kernels, run_pipeline(): pl.pallas_call(functools.partial(pipeline_kernel, n_stage, n_data, n_chun...  956 us
    dot_general x4, matrix products, dot(): return lax.dot_general(a, b, dims, preferred_element_type=F32)  321 us
  transfers between devices with their start and end apart: 2, of which 0 were waited for; matrix products, arithmetic and copies ran while one was open for 13% of the time, Pallas kernels for 0%

profile of v2, /device:TPU:0, one launch (start us, length us, event | category | flops | bytes accessed | tf_op | source)
XLA Modules:
  0.0 1281.0 jit_solution(1881063588951241419)
XLA Ops:
  0.6 956.0 %pipeline.1 = (bf16[4096,2048]{1,0:T(8,128)(2,1)}, bf16[4096,8192]{1,0:T(8,128)(2,1)}, f32[4096,8192]{1,0:T(8,128)}, bf16[4096,8192]{1,0:T(8,128)(2,1)}, bf16[4096,2048]{1,0:T(8,128)(2,1)}, /*index=5*/f32[8,512]{1,0:T(8,128)}) custom-call(bf16[4096,2048]{1,0:T(8,128)(2,1)} %bitcast.16, bf16[4096,2048]{1,0:T(8,128)(2,1)} %bitcast.17, ...), custom_call_target="tpu_custom_call" | custom-call | flops 549755813888 | bytes 1073741824 | tf_op jit(solution)/shard_map/pipeline/pallas_call | solution.py:472
  956.6 79.4 %fusion.3 = f32[1024,8192]{1,0:T(8,128)} fusion(bf16[4096,8192]{1,0:T(8,128)(2,1)} %get-tuple-element.10, bf16[4096,2048]{1,0:T(8,128)(2,1)} %get-tuple-element.9, s32[]{:T(128)S(6)} %select_n.9), kind=kOutput, calls=%fused_computation.5 | convolution fusion | flops 68719476736 | bytes 109051904 | tf_op jit(solution)/shard_map/dot_general | solution.py:25
  1036.0 0.0 collective-permute-start
  1036.0 0.0 copy-start
  1036.0 79.6 %fusion = f32[8192,1024]{1,0:T(8,128)} fusion(bf16[4096,8192]{1,0:T(8,128)(2,1)} %get-tuple-element.11, bf16[4096,2048]{1,0:T(8,128)(2,1)} %get-tuple-element.12, s32[]{:T(128)S(6)} %select_n.9), kind=kOutput, calls=%fused_computation.2 | convolution fusion | flops 68719476736 | bytes 109051904 | tf_op jit(solution)/shard_map/dot_general | solution.py:25
  1115.6 0.5 collective-permute-start.1
  1116.1 0.0 copy-done
  1116.1 0.6 reduce_sum.9
  1117.4 0.0 collective-permute-done
  1117.4 81.0 %add_bitcast_fusion.1 = f32[1,1024,8192]{2,1,0:T(8,128)} fusion(f32[1024,8192]{1,0:T(8,128)} %collective-permute-done, bf16[4096,8192]{1,0:T(8,128)(2,1)} %get-tuple-element.10, bf16[4096,2048]{1,0:T(8,128)(2,1)} %get-tuple-element.9, s32[]{:T(128)S(6)} %select_n.8), kind=kOutput, calls=%fused_computation.1 | convolution fusion | flops 68727865344 | bytes 142606336 | tf_op jit(solution)/shard_map/dot_general | solution.py:25
  1198.4 0.0 collective-permute-done.1
  1198.4 81.0 %add_bitcast_fusion = f32[1,8192,1024]{2,1,0:T(8,128)} fusion(f32[8192,1024]{1,0:T(8,128)} %collective-permute-done.1, bf16[4096,8192]{1,0:T(8,128)(2,1)} %get-tuple-element.11, bf16[4096,2048]{1,0:T(8,128)(2,1)} %get-tuple-element.12, s32[]{:T(128)S(6)} %select_n.8), kind=kOutput, calls=%fused_computation | convolution fusion | flops 68727865344 | bytes 142606336 | tf_op jit(solution)/shard_map/dot_general | solution.py:25
Async XLA Ops:
  1036.0 81.3 %collective-permute-start = (f32[1024,8192]{1,0:T(8,128)}, f32[1024,8192]{1,0:T(8,128)}, u32[]{:S(2)}, u32[]{:S(2)}) collective-permute-start(f32[1024,8192]{1,0:T(8,128)} %fusion.3), channel_id=1, source_target_pairs={{0,1},{1,0},{2,3},{3,2},{4,5},{5,4},{6,7},{7,6}} | collective-permute-start | bytes 100663304 | tf_op jit(solution)/shard_map/ppermute | solution.py:511
  1036.0 80.1 %copy-start = (f32[8,512]{1,0:T(8,128)S(1)}, f32[8,512]{1,0:T(8,128)}, u32[]{:S(2)}) copy-start(f32[8,512]{1,0:T(8,128)} %get-tuple-element.8) | copy-start | bytes 49156
  1115.6 82.7 %collective-permute-start.1 = (f32[8192,1024]{1,0:T(8,128)}, f32[8192,1024]{1,0:T(8,128)}, u32[]{:S(2)}, u32[]{:S(2)}) collective-permute-start(f32[8192,1024]{1,0:T(8,128)} %fusion), channel_id=1, source_target_pairs={{0,1},{1,0},{2,3},{3,2},{4,5},{5,4},{6,7},{7,6}} | collective-permute-start | bytes 100663304 | tf_op jit(solution)/shard_map/ppermute | solution.py:512

commit v3 on v2

--- a/solution.py
+++ b/solution.py
@@ -25,12 +25,22 @@
     return lax.dot_general(a, b, dims, preferred_element_type=F32)
 
 
+N_BLOCK = 16
+
+
+def early_plan(s):
+    n_unit = jnp.where(s == 0, 44, jnp.where(s == 1, 34, jnp.where(s == 2, 16, 0)))
+    after = jnp.where(s == 2, 10, 8)
+    each = jnp.where(s == 0, 44, jnp.where(s == 1, 5, 4))
+    return n_unit, after, each
+
+
 def pipeline_kernel(n_stage, n_data, n_chunk, inv_total,
                     x, y, w1, w2,
-                    hs, gs, ds, qs, es, loss_out,
+                    hs, gs, ds, qs, es, up_part, down_part, loss_out,
                     w1r, w2r, ring, gq, dbuf, inb, out, loss_acc, lbuf,
                     w1_sem, w2_sem, ring_sem, d_sem, gq_sem, in_sem, o_send,
-                    h_recv, e_recv, y_sem, st_sem, l_send, l_recv):
+                    h_recv, e_recv, y_sem, st_sem, l_send, l_recv, held_sem, tile_sem, part_sem):
     s = lax.axis_index('stage')
     peer = n_data - 1 - lax.axis_index('data')
     first = s == 0
@@ -168,9 +178,9 @@
             o = lax.rem(k, 2)
             copy(out.at[o], out.at[o], o_send.at[o]).wait()
 
-    def gelu_tile(q, c):
+    def gelu_tile(q, c, lo, hi):
         for r in range(0, ROWS, 16):
-            for z in range(0, CT, 256):
+            for z in range(lo, hi, 256):
                 u = dbuf[q, pl.ds(r, 16), pl.ds(z, 256)]
                 u2 = u * u
                 h = 0.5 * jnp.tanh(u * (C0 + (C0 * C1) * u2)) + 0.5
@@ -209,10 +219,16 @@
 
             wait_ring(j)
             jp = jnp.maximum(j - 1, 0)
-            dbuf[d_out_slot(j, 0)] = dot(inb[p], w1r[:, cols(j, CT)], NN)
-            gelu_tile(2 + lax.rem(j + 2, 3), half + jp * CT)
-            dbuf[d_out_slot(j, 1)] = dot(inb[p], ring[j], NN)
-            gelu_tile(d_out_slot(j, 0), j * CT)
+            res, stm, old = d_out_slot(j, 0), d_out_slot(j, 1), 2 + lax.rem(j + 2, 3)
+            old_at, res_at = half + jp * CT, j * CT
+            dbuf[res, :, pl.ds(0, DT)] = dot(inb[p], w1r[:, cols(2 * j, DT)], NN)
+            gelu_tile(old, old_at, 0, 768)
+            dbuf[res, :, pl.ds(DT, DT)] = dot(inb[p], w1r[:, cols(2 * j + 1, DT)], NN)
+            gelu_tile(old, old_at, 768, CT)
+            gelu_tile(res, res_at, 0, 512)
+            dbuf[stm, :, pl.ds(0, DT)] = dot(inb[p], ring[j, :, pl.ds(0, DT)], NN)
+            gelu_tile(res, res_at, 512, CT)
+            dbuf[stm, :, pl.ds(DT, DT)] = dot(inb[p], ring[j, :, pl.ds(DT, DT)], NN)
 
             @pl.when(j >= 1)
             def _():
@@ -252,7 +268,7 @@
                 v = dot(gq[:, pl.ds(0, half)], w2r[:, cols(j, DT)], NN)
                 if j == 0:
                     dbuf[3, :, pl.ds(0, DT)] = v
-                    gelu_tile(2, half + 3 * CT)
+                    gelu_tile(2, half + 3 * CT, 0, CT)
                     v = dbuf[3, :, pl.ds(0, DT)]
                 v = v + dot(gq[:, pl.ds(half, 2048)], ring[j, :, pl.ds(0, DT)], NN)
                 v = v + dot(gq[:, pl.ds(half + 2048, 2048)], ring[j, :, pl.ds(DT, DT)], NN)
@@ -345,6 +361,101 @@
 
             lax.fori_loop(0, 2, step2, 0)
 
+    def early_units(i):
+        n_unit, after, each = early_plan(s)
+        lo = jnp.clip((i - after) * each, 0, n_unit)
+        return lo, jnp.where(i >= after, jnp.clip((i - after + 1) * each, 0, n_unit), lo)
+
+    def early(i):
+        lo, hi = early_units(i)
+        n_tok = ring.shape[1]
+
+        def tile(u, start):
+            dst = ring.at[3, :, pl.ds(pl.multiple_of(lax.rem(u, 2) * DT, DT), DT)]
+            sem = tile_sem.at[lax.rem(u, 2)]
+            if not start:
+                copy(dst, dst, sem).wait()
+                return
+            b = lax.rem(u, N_BLOCK)
+
+            @pl.when(u < 2 * N_BLOCK)
+            def _():
+                copy(gs.at[pl.ds(0, n_tok), cols(b, DT)], dst, sem).start()
+
+            @pl.when(u >= 2 * N_BLOCK)
+            def _():
+                copy(qs.at[pl.ds(0, n_tok), cols(b, DT)], dst, sem).start()
+
+        def part_slot(t):
+            z = lax.rem(t, 3)
+            return jnp.where(z == 2, 4, z + 1)
+
+        def wait_part(t):
+            q = part_slot(t)
+            copy(dbuf.at[q], dbuf.at[q], part_sem.at[lax.rem(t, 3)]).wait()
+
+        def unit(u, carry):
+            hf = lax.rem(u // N_BLOCK, 2)
+            b = lax.rem(u, N_BLOCK)
+            c0 = lax.rem(u, 2) * DT
+
+            @pl.when((u == lo) | (b == 0))
+            def _():
+                @pl.when(u < 2 * N_BLOCK)
+                def _():
+                    copy(es.at[pl.ds(0, n_tok), cols(hf, CT)], ring.at[2], held_sem).start()
+
+                @pl.when(u >= 2 * N_BLOCK)
+                def _():
+                    copy(hs.at[pl.ds(0, n_tok), cols(hf, CT)], ring.at[2], held_sem).start()
+
+            @pl.when(u == lo)
+            def _():
+                tile(u, True)
+
+            @pl.when(u + 1 < hi)
+            def _():
+                tile(u + 1, True)
+
+            @pl.when((u == lo) | (b == 0))
+            def _():
+                copy(ring.at[2], ring.at[2], held_sem).wait()
+
+            tile(u, False)
+            for z in range(2):
+                t = 2 * (u - lo) + z
+                q = part_slot(t)
+
+                @pl.when(t >= 3)
+                def _():
+                    wait_part(t)
+
+                @pl.when(u < 2 * N_BLOCK)
+                def _():
+                    dbuf[q] = dot(ring[3, :, pl.ds(pl.multiple_of(c0 + z * ROWS, ROWS), ROWS)], ring[2], TN)
+                    copy(dbuf.at[q], down_part.at[cols(2 * b + z, ROWS), cols(hf, CT)], part_sem.at[lax.rem(t, 3)]).start()
+
+                @pl.when(u >= 2 * N_BLOCK)
+                def _():
+                    for a in range(2):
+                        r = 2 * z + a
+                        dbuf[q, :, pl.ds(a * DT, DT)] = dot(ring[2, :, pl.ds(r * ROWS, ROWS)], ring[3, :, pl.ds(pl.multiple_of(c0, DT), DT)], TN)
+                    for a in range(2):
+                        r = 2 * z + a
+                        copy(dbuf.at[q, :, pl.ds(a * DT, DT)], up_part.at[cols(4 * hf + r, ROWS), cols(b, DT)], part_sem.at[lax.rem(t, 3)]).start()
+            return carry
+
+        lax.fori_loop(lo, hi, unit, 0)
+
+        @pl.when(hi > lo)
+        def _():
+            wait_part(2 * (hi - lo) - 1)
+            wait_part(2 * (hi - lo) - 2)
+
+        @pl.when(hi > lo + 1)
+        def _():
+            wait_part(2 * (hi - lo) - 3)
+
     barrier = pltpu.get_barrier_semaphore()
 
     def hello(**to):
@@ -422,6 +533,10 @@
         @pl.when((is_f & first) | (jnp.logical_not(is_f) & last))
         def _():
             copy(inb.at[p], inb.at[p], st_sem).wait()
+
+        @pl.when(jnp.logical_not(is_f))
+        def _():
+            early(i)
 
         return carry
 
@@ -472,9 +587,9 @@
     return pl.pallas_call(
         functools.partial(pipeline_kernel, n_stage, n_data, n_chunk, 1.0 / (n_data * n_row)),
         out_shape=(out((n_row, width), BF16), out((n_row, ffn), BF16), out((n_row, ffn), F32),
-                   out((n_row, ffn), BF16), out((n_row, width), BF16), out((8, DT), F32)),
+                   out((n_row, ffn), BF16), out((n_row, width), BF16), out((width, ffn), F32), out((ffn, width), F32), out((8, DT), F32)),
         in_specs=[hbm] * 4,
-        out_specs=(hbm,) * 5 + (pl.BlockSpec(memory_space=pltpu.VMEM),),
+        out_specs=(hbm,) * 7 + (pl.BlockSpec(memory_space=pltpu.VMEM),),
         scratch_shapes=[
             pltpu.VMEM((width, half), BF16), pltpu.VMEM((half, width), BF16),
             pltpu.VMEM((RING, width, CT), BF16), pltpu.VMEM((ROWS, ffn), BF16),
@@ -482,7 +597,7 @@
             pltpu.VMEM((2, ROWS, width), BF16), pltpu.VMEM((16, DT), F32),
             pltpu.VMEM((3, 8, DT), F32),
             dma((NSTEP,)), dma((NSTEP,)), dma((RING,)), dma((5,)), dma, dma((2,)), dma((2,)),
-            dma((n_chunk,)), dma((n_chunk,)), dma, dma, dma((2,)), dma((2,)),
+            dma((n_chunk,)), dma((n_chunk,)), dma, dma, dma((2,)), dma((2,)), dma, dma((2,)), dma((3,)),
         ],
         compiler_params=pltpu.CompilerParams(collective_id=0, has_side_effects=True, vmem_limit_bytes=67043328),
         cost_estimate=pl.CostEstimate(flops=flops, bytes_accessed=1 << 30, transcendentals=n_row * ffn),
@@ -490,6 +605,57 @@
     )(x, y, w1, w2)
 
 
+def grad_kernel(up, sc, held, lo, hi, part, *rest):
+    got, o = rest if len(rest) == 2 else (None, rest[0])
+    n = hi.shape[0]
+
+    def product(rows_, tile):
+        return dot(held[rows_, :], tile[...], TN) if up else dot(tile[...], held[rows_, :], TN)
+
+    def finish(v):
+        o[...] = v if got is None else v + got[...]
+
+    @pl.when(pl.program_id(0) < sc[1])
+    def _():
+        finish(product(pl.ds(n, n), hi) + part[...])
+
+    @pl.when(pl.program_id(0) >= sc[1])
+    def _():
+        finish(product(pl.ds(0, n), lo) + product(pl.ds(n, n), hi))
+
+
+def weight_grad(up, held, streamed, part, side, n_done, got=None):
+    n_row, width = held.shape
+    half = width // 2
+    n_tok = n_row // 2
+    ffn = streamed.shape[1]
+    shape = (half, DT) if up else (DT, half)
+
+    def at(i, j):
+        return (j, i) if up else (i, j)
+
+    specs = [
+        pl.BlockSpec((n_row, half), lambda b, sc: (0, sc[0])),
+        pl.BlockSpec((n_tok, DT), lambda b, sc: (0, jnp.maximum(b, jnp.minimum(sc[1], N_BLOCK - 1)))),
+        pl.BlockSpec((n_tok, DT), lambda b, sc: (1, b)),
+        pl.BlockSpec(shape, lambda b, sc: at(jnp.minimum(b, jnp.maximum(sc[1] - 1, 0)), sc[0])),
+    ]
+    args = [held, streamed, streamed, part]
+    if got is not None:
+        specs.append(pl.BlockSpec(shape, lambda b, sc: at(b, 0)))
+        args.append(got)
+    return pl.pallas_call(
+        functools.partial(grad_kernel, up),
+        out_shape=jax.ShapeDtypeStruct((half, ffn) if up else (ffn, half), F32),
+        grid_spec=pltpu.PrefetchScalarGridSpec(
+            num_scalar_prefetch=1, grid=(ffn // DT,), in_specs=specs,
+            out_specs=pl.BlockSpec(shape, lambda b, sc: at(b, 0))),
+        compiler_params=pltpu.CompilerParams(dimension_semantics=('arbitrary',), vmem_limit_bytes=60 * 2**20),
+        cost_estimate=pl.CostEstimate(flops=2 * n_row * half * ffn, bytes_accessed=2 * n_row * ffn + 8 * half * ffn, transcendentals=0),
+        name='grad_up' if up else 'grad_down',
+    )(jnp.stack([side, n_done]).astype(jnp.int32), *args)
+
+
 def solution(mesh):
     n_stage = mesh.shape['stage']
     n_data = mesh.shape['data']
@@ -499,19 +665,22 @@
         n_row = n_micro * n_tok
         x = inputs.reshape(n_row, width)
         y = targets.reshape(n_row, width)
-        hs, gs, _, qs, es, loss = run_pipeline(n_stage, n_data, x, y, w_up, w_down)
-        half = width // n_data
-        mine = lax.axis_index('data') * half
-        other = (n_data - 1) * half - mine
+        hs, gs, _, qs, es, up_part, down_part, loss = run_pipeline(n_stage, n_data, x, y, w_up, w_down)
+        n_unit, _, _ = early_plan(lax.axis_index('stage'))
+        mine = lax.axis_index('data')
+        other = n_data - 1 - mine
         swap = [(0, 1), (1, 0)]
 
-        def part(a, at):
-            return lax.dynamic_slice_in_dim(a, at, half, 1)
-
-        up_other = lax.ppermute(dot(part(hs, other), qs, TN), 'data', swap)
-        down_other = lax.ppermute(dot(gs, part(es, other), TN), 'data', swap)
-        g_up = dot(part(hs, mine), qs, TN) + up_other
-        g_down = dot(gs, part(es, mine), TN) + down_other
+        def grad(up, side, got=None):
+            done = jnp.clip(n_unit - N_BLOCK * (side + (2 if up else 0)), 0, N_BLOCK)
+            if up:
+                return weight_grad(True, hs, qs, up_part, side, done, got)
+            return weight_grad(False, es, gs, down_part, side, done, got)
+
+        up_other = lax.ppermute(grad(True, other), 'data', swap)
+        down_other = lax.ppermute(grad(False, other), 'data', swap)
+        g_up = grad(True, mine, up_other)
+        g_down = grad(False, mine, down_other)
         loss_total = jnp.sum(loss) * (0.5 / (n_data * n_row))
         return loss_total, g_up[None], g_down[None]
 

time: 1290 us -> 1290 us (level)
  the two profiles are of different devices: /device:TPU:0 before, /device:TPU:1 now
where the time goes in v3:
time: 1290 us; the launch traced here: 1280 us
  Pallas kernels  1250 us (97%)
  starting transfers between devices  24.9 us (2%)
    pallas_call x1, Pallas kernels, run_pipeline(): pl.pallas_call(functools.partial(pipeline_kernel, n_stage, n_data, n_chun...  998 us
    pallas_call x4, Pallas kernels, weight_grad(): pl.pallas_call(functools.partial(grad_kernel, up), out_shape=jax.ShapeDty...  251 us
  transfers between devices with their start and end apart: 2, of which 0 were waited for; matrix products, arithmetic and copies ran while one was open for 0% of the time, Pallas kernels for 10%

profile of v3, /device:TPU:1, one launch (start us, length us, event | category | flops | bytes accessed | tf_op | source)
XLA Modules:
  0.0 1279.2 jit_solution(7352243546061766024)
XLA Ops:
  0.7 0.6 pad_add_fusion.1.sc
  1.3 997.6 %pipeline.1 = (bf16[4096,2048]{1,0:T(8,128)(2,1)}, bf16[4096,8192]{1,0:T(8,128)(2,1)}, f32[4096,8192]{1,0:T(8,128)}, bf16[4096,8192]{1,0:T(8,128)(2,1)}, bf16[40...) custom-call(bf16[4096,2048]{1,0:T(8,128)(2,1)} %bitcast.12, ...), custom_call_target="tpu_custom_call" | custom-call | flops 549755813888 | bytes 1073741824 | tf_op jit(solution)/shard_map/pipeline/pallas_call | solution.py:587
  998.9 58.5 %grad_up.2 = f32[1024,8192]{1,0:T(8,128)} custom-call(s32[2]{0:T(128)} %pad_add_fusion.1.sc, bf16[4096,2048]{1,0:T(8,128)(2,1)} %get-tuple-element.11.held, bf16[4096,8192]{1,0:T(8,128)(2,1)} %get-tuple-element.12.lo.hi, bf16[4096,8192]{1,0:T(8,128)(2,1)} %get-tuple-element.12.lo.hi, f32[2048,8192]{1,0:T(8,128)} %get-tuple-element.13.part), custom_call_target="tpu_custom_call" | custom-call | flops 68719476736 | bytes 134217728 | tf_op jit(solution)/shard_map/grad_up/pallas_call | solution.py:647
  1057.4 24.9 %collective-permute-start = (f32[1024,8192]{1,0:T(8,128)}, f32[1024,8192]{1,0:T(8,128)}, u32[]{:S(2)}, u32[]{:S(2)}) collective-permute-start(f32[1024,8192]{1,0:T(8,128)} %grad_up.2), channel_id=1, source_target_pairs={{0,1},{1,0},{2,3},{3,2},{4,5},{5,4},{6,7},{7,6}} | collective-permute-start | bytes 100663304 | tf_op jit(solution)/shard_map/ppermute | solution.py:680
  1082.3 0.6 pad_add_fusion.3.sc
  1082.9 0.0 copy-start
  1082.9 51.1 %grad_down.2 = f32[8192,1024]{1,0:T(8,128)} custom-call(s32[2]{0:T(128)} %pad_add_fusion.3.sc, bf16[4096,2048]{1,0:T(8,128)(2,1)} %get-tuple-element.14.held, bf16[4096,8192]{1,0:T(8,128)(2,1)} %get-tuple-element.15.lo.hi, bf16[4096,8192]{1,0:T(8,128)(2,1)} %get-tuple-element.15.lo.hi, f32[8192,2048]{1,0:T(8,128)} %get-tuple-element.16.part), custom_call_target="tpu_custom_call" | custom-call | flops 68719476736 | bytes 134217728 | tf_op jit(solution)/shard_map/grad_down/pallas_call | solution.py:647
  1134.0 0.0 collective-permute-start.1
  1134.0 0.0 copy-done
  1134.0 0.6 reduce_sum.9
  1135.3 0.7 pad_add_fusion.sc
  1135.9 0.6 pad_add_fusion.2.sc
  1136.6 0.0 collective-permute-done.rest_0_
  1136.6 82.2 %grad_up.3 = f32[1024,8192]{1,0:T(8,128)} custom-call(s32[2]{0:T(128)} %pad_add_fusion.sc, bf16[4096,2048]{1,0:T(8,128)(2,1)} %get-tuple-element.11.held, bf16[4096,8192]{1,0:T(8,128)(2,1)} %get-tuple-element.12.lo.hi, bf16[4096,8192]{1,0:T(8,128)(2,1)} %get-tuple-element.12.lo.hi, f32[2048,8192]{1,0:T(8,128)} %get-tuple-element.13.part, ...), custom_call_target="tpu_custom_call" | custom-call | flops 68719476736 | bytes 134217728 | tf_op jit(solution)/shard_map/grad_up/pallas_call | solution.py:647
  1218.7 0.0 collective-permute-done.1.rest_0_
  1218.7 58.9 %grad_down.3 = f32[8192,1024]{1,0:T(8,128)} custom-call(s32[2]{0:T(128)} %pad_add_fusion.2.sc, bf16[4096,2048]{1,0:T(8,128)(2,1)} %get-tuple-element.14.held, bf16[4096,8192]{1,0:T(8,128)(2,1)} %get-tuple-element.15.lo.hi, bf16[4096,8192]{1,0:T(8,128)(2,1)} %get-tuple-element.15.lo.hi, f32[8192,2048]{1,0:T(8,128)} %get-tuple-element.16.part, ...), custom_call_target="tpu_custom_call" | custom-call | flops 68719476736 | bytes 134217728 | tf_op jit(solution)/shard_map/grad_down/pallas_call | solution.py:647
Async XLA Ops:
  1057.4 79.2 %collective-permute-start = (f32[1024,8192]{1,0:T(8,128)}, f32[1024,8192]{1,0:T(8,128)}, u32[]{:S(2)}, u32[]{:S(2)}) collective-permute-start(f32[1024,8192]{1,0:T(8,128)} %grad_up.2), channel_id=1, source_target_pairs={{0,1},{1,0},{2,3},{3,2},{4,5},{5,4},{6,7},{7,6}} | collective-permute-start | bytes 100663304 | tf_op jit(solution)/shard_map/ppermute | solution.py:680
  1082.9 51.1 %copy-start = (f32[8,512]{1,0:T(8,128)S(1)}, f32[8,512]{1,0:T(8,128)}, u32[]{:S(2)}) copy-start(f32[8,512]{1,0:T(8,128)} %get-tuple-element.10) | copy-start | bytes 49156
  1134.0 84.7 %collective-permute-start.1 = (f32[8192,1024]{1,0:T(8,128)}, f32[8192,1024]{1,0:T(8,128)}, u32[]{:S(2)}, u32[]{:S(2)}) collective-permute-start(f32[8192,1024]{1,0:T(8,128)} %grad_down.2), channel_id=1, source_target_pairs={{0,1},{1,0},{2,3},{3,2},{4,5},{5,4},{6,7},{7,6}} | collective-permute-start | bytes 100663304 | tf_op jit(solution)/shard_map/ppermute | solution.py:681

commit v4 on v3

--- a/solution.py
+++ b/solution.py
@@ -29,9 +29,9 @@
 
 
 def early_plan(s):
-    n_unit = jnp.where(s == 0, 44, jnp.where(s == 1, 34, jnp.where(s == 2, 16, 0)))
+    n_unit = jnp.where(s == 0, 60, jnp.where(s == 1, 34, jnp.where(s == 2, 16, 0)))
     after = jnp.where(s == 2, 10, 8)
-    each = jnp.where(s == 0, 44, jnp.where(s == 1, 5, 4))
+    each = jnp.where(s == 0, 60, jnp.where(s == 1, 6, 4))
     return n_unit, after, each
 
 
@@ -47,7 +47,7 @@
     last = s == n_stage - 1
     half = w1r.shape[1]
     n_slot = 2 * n_chunk
-    warm = n_chunk - 5 * s
+    warm = jnp.where(first, n_chunk, jnp.where(last, 1, 12 - 4 * s))
 
     def order(k):
         j = jnp.maximum(k - warm, 0)

time: 1290 us -> 1240 us (0.961)
  the two profiles are of different devices: /device:TPU:1 before, /device:TPU:3 now
where the time goes in v4:
time: 1240 us; the launch traced here: 1230 us
  Pallas kernels  1210 us (98%)
    pallas_call x1, Pallas kernels, run_pipeline(): pl.pallas_call(functools.partial(pipeline_kernel, n_stage, n_data, n_chun...  945 us
    pallas_call x4, Pallas kernels, weight_grad(): pl.pallas_call(functools.partial(grad_kernel, up), out_shape=jax.ShapeDty...  269 us
  transfers between devices with their start and end apart: 2, of which 0 were waited for; matrix products, arithmetic and copies ran while one was open for 0% of the time, Pallas kernels for 11%

profile of v4, /device:TPU:3, one launch (start us, length us, event | category | flops | bytes accessed | tf_op | source)
XLA Modules:
  0.0 1227.8 jit_solution(2513985112730602340)
XLA Ops:
  0.7 0.6 pad_add_fusion.1.sc
  1.3 944.5 %pipeline.1 = (bf16[4096,2048]{1,0:T(8,128)(2,1)}, bf16[4096,8192]{1,0:T(8,128)(2,1)}, f32[4096,8192]{1,0:T(8,128)}, bf16[4096,8192]{1,0:T(8,128)(2,1)}, bf16[40...) custom-call(bf16[4096,2048]{1,0:T(8,128)(2,1)} %bitcast.12, ...), custom_call_target="tpu_custom_call" | custom-call | flops 549755813888 | bytes 1073741824 | tf_op jit(solution)/shard_map/pipeline/pallas_call | solution.py:587
  945.8 76.9 %grad_up.2 = f32[1024,8192]{1,0:T(8,128)} custom-call(s32[2]{0:T(128)} %pad_add_fusion.1.sc, bf16[4096,2048]{1,0:T(8,128)(2,1)} %get-tuple-element.11.held, bf16[4096,8192]{1,0:T(8,128)(2,1)} %get-tuple-element.12.lo.hi, bf16[4096,8192]{1,0:T(8,128)(2,1)} %get-tuple-element.12.lo.hi, f32[2048,8192]{1,0:T(8,128)} %get-tuple-element.13.part), custom_call_target="tpu_custom_call" | custom-call | flops 68719476736 | bytes 134217728 | tf_op jit(solution)/shard_map/grad_up/pallas_call | solution.py:647
  1022.7 8.2 collective-permute-start
  1030.9 0.6 pad_add_fusion.3.sc
  1031.6 0.0 copy-start
  1031.6 51.1 %grad_down.2 = f32[8192,1024]{1,0:T(8,128)} custom-call(s32[2]{0:T(128)} %pad_add_fusion.3.sc, bf16[4096,2048]{1,0:T(8,128)(2,1)} %get-tuple-element.14.held, bf16[4096,8192]{1,0:T(8,128)(2,1)} %get-tuple-element.15.lo.hi, bf16[4096,8192]{1,0:T(8,128)(2,1)} %get-tuple-element.15.lo.hi, f32[8192,2048]{1,0:T(8,128)} %get-tuple-element.16.part), custom_call_target="tpu_custom_call" | custom-call | flops 68719476736 | bytes 134217728 | tf_op jit(solution)/shard_map/grad_down/pallas_call | solution.py:647
  1082.7 0.0 collective-permute-start.1
  1082.7 0.0 copy-done
  1082.7 0.6 reduce_sum.9
  1084.0 0.7 pad_add_fusion.sc
  1084.6 0.6 pad_add_fusion.2.sc
  1085.2 0.0 collective-permute-done.rest_0_
  1085.2 82.2 %grad_up.3 = f32[1024,8192]{1,0:T(8,128)} custom-call(s32[2]{0:T(128)} %pad_add_fusion.sc, bf16[4096,2048]{1,0:T(8,128)(2,1)} %get-tuple-element.11.held, bf16[4096,8192]{1,0:T(8,128)(2,1)} %get-tuple-element.12.lo.hi, bf16[4096,8192]{1,0:T(8,128)(2,1)} %get-tuple-element.12.lo.hi, f32[2048,8192]{1,0:T(8,128)} %get-tuple-element.13.part, ...), custom_call_target="tpu_custom_call" | custom-call | flops 68719476736 | bytes 134217728 | tf_op jit(solution)/shard_map/grad_up/pallas_call | solution.py:647
  1167.4 0.0 collective-permute-done.1.rest_0_
  1167.4 58.9 %grad_down.3 = f32[8192,1024]{1,0:T(8,128)} custom-call(s32[2]{0:T(128)} %pad_add_fusion.2.sc, bf16[4096,2048]{1,0:T(8,128)(2,1)} %get-tuple-element.14.held, bf16[4096,8192]{1,0:T(8,128)(2,1)} %get-tuple-element.15.lo.hi, bf16[4096,8192]{1,0:T(8,128)(2,1)} %get-tuple-element.15.lo.hi, f32[8192,2048]{1,0:T(8,128)} %get-tuple-element.16.part, ...), custom_call_target="tpu_custom_call" | custom-call | flops 68719476736 | bytes 134217728 | tf_op jit(solution)/shard_map/grad_down/pallas_call | solution.py:647
Async XLA Ops:
  1022.7 62.5 %collective-permute-start = (f32[1024,8192]{1,0:T(8,128)}, f32[1024,8192]{1,0:T(8,128)}, u32[]{:S(2)}, u32[]{:S(2)}) collective-permute-start(f32[1024,8192]{1,0:T(8,128)} %grad_up.2), channel_id=1, source_target_pairs={{0,1},{1,0},{2,3},{3,2},{4,5},{5,4},{6,7},{7,6}} | collective-permute-start | bytes 100663304 | tf_op jit(solution)/shard_map/ppermute | solution.py:680
  1031.6 51.1 %copy-start = (f32[8,512]{1,0:T(8,128)S(1)}, f32[8,512]{1,0:T(8,128)}, u32[]{:S(2)}) copy-start(f32[8,512]{1,0:T(8,128)} %get-tuple-element.10) | copy-start | bytes 49156
  1082.7 84.7 %collective-permute-start.1 = (f32[8192,1024]{1,0:T(8,128)}, f32[8192,1024]{1,0:T(8,128)}, u32[]{:S(2)}, u32[]{:S(2)}) collective-permute-start(f32[8192,1024]{1,0:T(8,128)} %grad_down.2), channel_id=1, source_target_pairs={{0,1},{1,0},{2,3},{3,2},{4,5},{5,4},{6,7},{7,6}} | collective-permute-start | bytes 100663304 | tf_op jit(solution)/shard_map/ppermute | solution.py:681

commit v5 on v4

--- a/solution.py
+++ b/solution.py
@@ -29,9 +29,9 @@
 
 
 def early_plan(s):
-    n_unit = jnp.where(s == 0, 60, jnp.where(s == 1, 34, jnp.where(s == 2, 16, 0)))
-    after = jnp.where(s == 2, 10, 8)
-    each = jnp.where(s == 0, 60, jnp.where(s == 1, 6, 4))
+    n_unit = jnp.where(s == 0, 60, jnp.where(s == 1, 32, jnp.where(s == 2, 16, 0)))
+    after = jnp.where(s == 2, 10, jnp.where(s == 1, 7, 8))
+    each = jnp.where(s == 0, 60, jnp.where(s == 1, 5, 4))
     return n_unit, after, each
 
 
@@ -123,7 +123,8 @@
         return is_f | jnp.logical_not(last)
 
     def ahead(k):
-        return (first | (k >= warm)) & (k < n_slot)
+        is_f, _ = order(k)
+        return is_f & (first | (last & (k >= warm))) & (k < n_slot)
 
     def load_in(k):
         is_f, i = order(k)

time: 1240 us -> 1230 us (level)
  the two profiles are of different devices: /device:TPU:3 before, /device:TPU:5 now
where the time goes in v5:
time: 1230 us; the launch traced here: 1220 us
  Pallas kernels  1180 us (96%)
  starting transfers between devices  33.3 us (3%)
    pallas_call x1, Pallas kernels, run_pipeline(): pl.pallas_call(functools.partial(pipeline_kernel, n_stage, n_data, n_chun...  883 us
    pallas_call x4, Pallas kernels, weight_grad(): pl.pallas_call(functools.partial(grad_kernel, up), out_shape=jax.ShapeDty...  296 us
    ppermute x1, starting transfers between devices, per_device(): down_other = lax.ppermute(grad(False, other), 'data', swap)  30.1 us
  transfers between devices with their start and end apart: 2, of which 0 were waited for; matrix products, arithmetic and copies ran while one was open for 0% of the time, Pallas kernels for 11%

profile of v5, /device:TPU:5, one launch (start us, length us, event | category | flops | bytes accessed | tf_op | source)
XLA Modules:
  0.0 1218.9 jit_solution(15165443377095401749)
XLA Ops:
  0.7 0.6 pad_add_fusion.1.sc
  1.3 883.2 %pipeline.1 = (bf16[4096,2048]{1,0:T(8,128)(2,1)}, bf16[4096,8192]{1,0:T(8,128)(2,1)}, f32[4096,8192]{1,0:T(8,128)}, bf16[4096,8192]{1,0:T(8,128)(2,1)}, bf16[40...) custom-call(bf16[4096,2048]{1,0:T(8,128)(2,1)} %bitcast.12, ...), custom_call_target="tpu_custom_call" | custom-call | flops 549755813888 | bytes 1073741824 | tf_op jit(solution)/shard_map/pipeline/pallas_call | solution.py:588
  884.5 81.2 %grad_up.2 = f32[1024,8192]{1,0:T(8,128)} custom-call(s32[2]{0:T(128)} %pad_add_fusion.1.sc, bf16[4096,2048]{1,0:T(8,128)(2,1)} %get-tuple-element.11.held, bf16[4096,8192]{1,0:T(8,128)(2,1)} %get-tuple-element.12.lo.hi, bf16[4096,8192]{1,0:T(8,128)(2,1)} %get-tuple-element.12.lo.hi, f32[2048,8192]{1,0:T(8,128)} %get-tuple-element.13.part), custom_call_target="tpu_custom_call" | custom-call | flops 68719476736 | bytes 134217728 | tf_op jit(solution)/shard_map/grad_up/pallas_call | solution.py:648
  965.7 3.2 collective-permute-start
  968.9 0.6 pad_add_fusion.3.sc
  969.5 0.0 copy-start
  969.5 51.1 %grad_down.2 = f32[8192,1024]{1,0:T(8,128)} custom-call(s32[2]{0:T(128)} %pad_add_fusion.3.sc, bf16[4096,2048]{1,0:T(8,128)(2,1)} %get-tuple-element.14.held, bf16[4096,8192]{1,0:T(8,128)(2,1)} %get-tuple-element.15.lo.hi, bf16[4096,8192]{1,0:T(8,128)(2,1)} %get-tuple-element.15.lo.hi, f32[8192,2048]{1,0:T(8,128)} %get-tuple-element.16.part), custom_call_target="tpu_custom_call" | custom-call | flops 68719476736 | bytes 134217728 | tf_op jit(solution)/shard_map/grad_down/pallas_call | solution.py:648
  1020.6 30.1 %collective-permute-start.1 = (f32[8192,1024]{1,0:T(8,128)}, f32[8192,1024]{1,0:T(8,128)}, u32[]{:S(2)}, u32[]{:S(2)}) collective-permute-start(f32[8192,1024]{1,0:T(8,128)} %grad_down.2), channel_id=1, source_target_pairs={{0,1},{1,0},{2,3},{3,2},{4,5},{5,4},{6,7},{7,6}} | collective-permute-start | bytes 100663304 | tf_op jit(solution)/shard_map/ppermute | solution.py:682
  1050.7 0.0 copy-done
  1050.8 0.6 reduce_sum.9
  1052.0 0.7 pad_add_fusion.sc
  1052.7 0.6 pad_add_fusion.2.sc
  1053.3 0.0 collective-permute-done.rest_0_
  1053.3 82.2 %grad_up.3 = f32[1024,8192]{1,0:T(8,128)} custom-call(s32[2]{0:T(128)} %pad_add_fusion.sc, bf16[4096,2048]{1,0:T(8,128)(2,1)} %get-tuple-element.11.held, bf16[4096,8192]{1,0:T(8,128)(2,1)} %get-tuple-element.12.lo.hi, bf16[4096,8192]{1,0:T(8,128)(2,1)} %get-tuple-element.12.lo.hi, f32[2048,8192]{1,0:T(8,128)} %get-tuple-element.13.part, ...), custom_call_target="tpu_custom_call" | custom-call | flops 68719476736 | bytes 134217728 | tf_op jit(solution)/shard_map/grad_up/pallas_call | solution.py:648
  1135.5 0.0 collective-permute-done.1.rest_0_
  1135.5 81.9 %grad_down.3 = f32[8192,1024]{1,0:T(8,128)} custom-call(s32[2]{0:T(128)} %pad_add_fusion.2.sc, bf16[4096,2048]{1,0:T(8,128)(2,1)} %get-tuple-element.14.held, bf16[4096,8192]{1,0:T(8,128)(2,1)} %get-tuple-element.15.lo.hi, bf16[4096,8192]{1,0:T(8,128)(2,1)} %get-tuple-element.15.lo.hi, f32[8192,2048]{1,0:T(8,128)} %get-tuple-element.16.part, ...), custom_call_target="tpu_custom_call" | custom-call | flops 68719476736 | bytes 134217728 | tf_op jit(solution)/shard_map/grad_down/pallas_call | solution.py:648
Async XLA Ops:
  965.7 87.6 %collective-permute-start = (f32[1024,8192]{1,0:T(8,128)}, f32[1024,8192]{1,0:T(8,128)}, u32[]{:S(2)}, u32[]{:S(2)}) collective-permute-start(f32[1024,8192]{1,0:T(8,128)} %grad_up.2), channel_id=1, source_target_pairs={{0,1},{1,0},{2,3},{3,2},{4,5},{5,4},{6,7},{7,6}} | collective-permute-start | bytes 100663304 | tf_op jit(solution)/shard_map/ppermute | solution.py:681
  969.5 81.3 %copy-start = (f32[8,512]{1,0:T(8,128)S(1)}, f32[8,512]{1,0:T(8,128)}, u32[]{:S(2)}) copy-start(f32[8,512]{1,0:T(8,128)} %get-tuple-element.10) | copy-start | bytes 49156
  1020.6 114.8 %collective-permute-start.1 = (f32[8192,1024]{1,0:T(8,128)}, f32[8192,1024]{1,0:T(8,128)}, u32[]{:S(2)}, u32[]{:S(2)}) collective-permute-start(f32[8192,1024]{1,0:T(8,128)} %grad_down.2), channel_id=1, source_target_pairs={{0,1},{1,0},{2,3},{3,2},{4,5},{5,4},{6,7},{7,6}} | collective-permute-start | bytes 100663304 | tf_op jit(solution)/shard_map/ppermute | solution.py:682

commit v6 on v5

--- a/solution.py
+++ b/solution.py
@@ -29,10 +29,11 @@
 
 
 def early_plan(s):
-    n_unit = jnp.where(s == 0, 60, jnp.where(s == 1, 32, jnp.where(s == 2, 16, 0)))
-    after = jnp.where(s == 2, 10, jnp.where(s == 1, 7, 8))
+    n_down = jnp.where(s < 2, N_BLOCK, jnp.where(s == 2, 6, 0))
+    n_up = jnp.where(s == 0, 14, 0)
+    after = jnp.where(s == 2, 12, 8)
     each = jnp.where(s == 0, 60, jnp.where(s == 1, 5, 4))
-    return n_unit, after, each
+    return n_down, n_up, after, each
 
 
 def pipeline_kernel(n_stage, n_data, n_chunk, inv_total,
@@ -363,13 +364,23 @@
             lax.fori_loop(0, 2, step2, 0)
 
     def early_units(i):
-        n_unit, after, each = early_plan(s)
+        n_down, n_up, after, each = early_plan(s)
+        n_unit = 2 * (n_down + n_up)
         lo = jnp.clip((i - after) * each, 0, n_unit)
         return lo, jnp.where(i >= after, jnp.clip((i - after + 1) * each, 0, n_unit), lo)
 
     def early(i):
         lo, hi = early_units(i)
         n_tok = ring.shape[1]
+        n_down, n_up, _, _ = early_plan(s)
+
+        def place(u):
+            down = u < 2 * n_down
+            v = jnp.where(down, u, u - 2 * n_down)
+            n = jnp.maximum(jnp.where(down, n_down, n_up), 1)
+            side = jnp.where(v >= n, 1, 0)
+            return down, side, v - n * side
+
 
         def tile(u, start):
             dst = ring.at[3, :, pl.ds(pl.multiple_of(lax.rem(u, 2) * DT, DT), DT)]
@@ -377,13 +388,13 @@
             if not start:
                 copy(dst, dst, sem).wait()
                 return
-            b = lax.rem(u, N_BLOCK)
-
-            @pl.when(u < 2 * N_BLOCK)
+            down, _, b = place(u)
+
+            @pl.when(down)
             def _():
                 copy(gs.at[pl.ds(0, n_tok), cols(b, DT)], dst, sem).start()
 
-            @pl.when(u >= 2 * N_BLOCK)
+            @pl.when(jnp.logical_not(down))
             def _():
                 copy(qs.at[pl.ds(0, n_tok), cols(b, DT)], dst, sem).start()
 
@@ -396,17 +407,16 @@
             copy(dbuf.at[q], dbuf.at[q], part_sem.at[lax.rem(t, 3)]).wait()
 
         def unit(u, carry):
-            hf = lax.rem(u // N_BLOCK, 2)
-            b = lax.rem(u, N_BLOCK)
+            down, hf, b = place(u)
             c0 = lax.rem(u, 2) * DT
 
             @pl.when((u == lo) | (b == 0))
             def _():
-                @pl.when(u < 2 * N_BLOCK)
+                @pl.when(down)
                 def _():
                     copy(es.at[pl.ds(0, n_tok), cols(hf, CT)], ring.at[2], held_sem).start()
 
-                @pl.when(u >= 2 * N_BLOCK)
+                @pl.when(jnp.logical_not(down))
                 def _():
                     copy(hs.at[pl.ds(0, n_tok), cols(hf, CT)], ring.at[2], held_sem).start()
 
@@ -431,12 +441,12 @@
                 def _():
                     wait_part(t)
 
-                @pl.when(u < 2 * N_BLOCK)
+                @pl.when(down)
                 def _():
                     dbuf[q] = dot(ring[3, :, pl.ds(pl.multiple_of(c0 + z * ROWS, ROWS), ROWS)], ring[2], TN)
                     copy(dbuf.at[q], down_part.at[cols(2 * b + z, ROWS), cols(hf, CT)], part_sem.at[lax.rem(t, 3)]).start()
 
-                @pl.when(u >= 2 * N_BLOCK)
+                @pl.when(jnp.logical_not(down))
                 def _():
                     for a in range(2):
                         r = 2 * z + a
@@ -667,16 +677,15 @@
         x = inputs.reshape(n_row, width)
         y = targets.reshape(n_row, width)
         hs, gs, _, qs, es, up_part, down_part, loss = run_pipeline(n_stage, n_data, x, y, w_up, w_down)
-        n_unit, _, _ = early_plan(lax.axis_index('stage'))
+        n_down, n_up, _, _ = early_plan(lax.axis_index('stage'))
         mine = lax.axis_index('data')
         other = n_data - 1 - mine
         swap = [(0, 1), (1, 0)]
 
         def grad(up, side, got=None):
-            done = jnp.clip(n_unit - N_BLOCK * (side + (2 if up else 0)), 0, N_BLOCK)
             if up:
-                return weight_grad(True, hs, qs, up_part, side, done, got)
-            return weight_grad(False, es, gs, down_part, side, done, got)
+                return weight_grad(True, hs, qs, up_part, side, n_up, got)
+            return weight_grad(False, es, gs, down_part, side, n_down, got)
 
         up_other = lax.ppermute(grad(True, other), 'data', swap)
         down_other = lax.ppermute(grad(False, other), 'data', swap)

time: 1230 us -> 1220 us (level)
  the two profiles are of different devices: /device:TPU:5 before, /device:TPU:3 now
where the time goes in v6:
time: 1220 us; the launch traced here: 1210 us
  Pallas kernels  1200 us (98%)
    pallas_call x1, Pallas kernels, run_pipeline(): pl.pallas_call(functools.partial(pipeline_kernel, n_stage, n_data, n_chun...  925 us
    pallas_call x4, Pallas kernels, weight_grad(): pl.pallas_call(functools.partial(grad_kernel, up), out_shape=jax.ShapeDty...  273 us
  transfers between devices with their start and end apart: 2, of which 0 were waited for; matrix products, arithmetic and copies ran while one was open for 0% of the time, Pallas kernels for 11%

profile of v6, /device:TPU:3, one launch (start us, length us, event | category | flops | bytes accessed | tf_op | source)
XLA Modules:
  0.0 1209.1 jit_solution(6264825754939675596)
XLA Ops:
  0.6 0.6 pad_add_fusion.sc
  1.2 925.3 %pipeline.1 = (bf16[4096,2048]{1,0:T(8,128)(2,1)}, bf16[4096,8192]{1,0:T(8,128)(2,1)}, f32[4096,8192]{1,0:T(8,128)}, bf16[4096,8192]{1,0:T(8,128)(2,1)}, bf16[40...) custom-call(bf16[4096,2048]{1,0:T(8,128)(2,1)} %bitcast.10, ...), custom_call_target="tpu_custom_call" | custom-call | flops 549755813888 | bytes 1073741824 | tf_op jit(solution)/shard_map/pipeline/pallas_call | solution.py:598
  926.5 81.2 %grad_up.2 = f32[1024,8192]{1,0:T(8,128)} custom-call(s32[2]{0:T(128)} %pad_add_fusion.sc, bf16[4096,2048]{1,0:T(8,128)(2,1)} %get-tuple-element.11.held, bf16[4096,8192]{1,0:T(8,128)(2,1)} %get-tuple-element.12.lo.hi, bf16[4096,8192]{1,0:T(8,128)(2,1)} %get-tuple-element.12.lo.hi, f32[2048,8192]{1,0:T(8,128)} %get-tuple-element.13.part), custom_call_target="tpu_custom_call" | custom-call | flops 68719476736 | bytes 134217728 | tf_op jit(solution)/shard_map/grad_up/pallas_call | solution.py:658
  1007.7 4.4 collective-permute-start
  1012.1 0.7 pad_add_fusion.3.sc
  1012.8 0.0 copy-start
  1012.8 51.1 %grad_down.2 = f32[8192,1024]{1,0:T(8,128)} custom-call(s32[2]{0:T(128)} %pad_add_fusion.3.sc, bf16[4096,2048]{1,0:T(8,128)(2,1)} %get-tuple-element.14.held, bf16[4096,8192]{1,0:T(8,128)(2,1)} %get-tuple-element.15.lo.hi, bf16[4096,8192]{1,0:T(8,128)(2,1)} %get-tuple-element.15.lo.hi, f32[8192,2048]{1,0:T(8,128)} %get-tuple-element.16.part), custom_call_target="tpu_custom_call" | custom-call | flops 68719476736 | bytes 134217728 | tf_op jit(solution)/shard_map/grad_down/pallas_call | solution.py:658
  1063.9 0.0 collective-permute-start.1
  1064.0 0.0 copy-done
  1064.0 0.6 reduce_sum.9
  1065.2 0.7 pad_add_fusion.1.sc
  1065.9 0.6 pad_add_fusion.2.sc
  1066.5 0.0 collective-permute-done.rest_0_
  1066.5 82.2 %grad_up.3 = f32[1024,8192]{1,0:T(8,128)} custom-call(s32[2]{0:T(128)} %pad_add_fusion.1.sc, bf16[4096,2048]{1,0:T(8,128)(2,1)} %get-tuple-element.11.held, bf16[4096,8192]{1,0:T(8,128)(2,1)} %get-tuple-element.12.lo.hi, bf16[4096,8192]{1,0:T(8,128)(2,1)} %get-tuple-element.12.lo.hi, f32[2048,8192]{1,0:T(8,128)} %get-tuple-element.13.part, ...), custom_call_target="tpu_custom_call" | custom-call | flops 68719476736 | bytes 134217728 | tf_op jit(solution)/shard_map/grad_up/pallas_call | solution.py:658
  1148.7 0.0 collective-permute-done.1.rest_0_
  1148.7 58.9 %grad_down.3 = f32[8192,1024]{1,0:T(8,128)} custom-call(s32[2]{0:T(128)} %pad_add_fusion.2.sc, bf16[4096,2048]{1,0:T(8,128)(2,1)} %get-tuple-element.14.held, bf16[4096,8192]{1,0:T(8,128)(2,1)} %get-tuple-element.15.lo.hi, bf16[4096,8192]{1,0:T(8,128)(2,1)} %get-tuple-element.15.lo.hi, f32[8192,2048]{1,0:T(8,128)} %get-tuple-element.16.part, ...), custom_call_target="tpu_custom_call" | custom-call | flops 68719476736 | bytes 134217728 | tf_op jit(solution)/shard_map/grad_down/pallas_call | solution.py:658
Async XLA Ops:
  1007.7 58.8 %collective-permute-start = (f32[1024,8192]{1,0:T(8,128)}, f32[1024,8192]{1,0:T(8,128)}, u32[]{:S(2)}, u32[]{:S(2)}) collective-permute-start(f32[1024,8192]{1,0:T(8,128)} %grad_up.2), channel_id=1, source_target_pairs={{0,1},{1,0},{2,3},{3,2},{4,5},{5,4},{6,7},{7,6}} | collective-permute-start | bytes 100663304 | tf_op jit(solution)/shard_map/ppermute | solution.py:690
  1012.8 51.1 %copy-start = (f32[8,512]{1,0:T(8,128)S(1)}, f32[8,512]{1,0:T(8,128)}, u32[]{:S(2)}) copy-start(f32[8,512]{1,0:T(8,128)} %get-tuple-element.10) | copy-start | bytes 49156
  1063.9 84.7 %collective-permute-start.1 = (f32[8192,1024]{1,0:T(8,128)}, f32[8192,1024]{1,0:T(8,128)}, u32[]{:S(2)}, u32[]{:S(2)}) collective-permute-start(f32[8192,1024]{1,0:T(8,128)} %grad_down.2), channel_id=1, source_target_pairs={{0,1},{1,0},{2,3},{3,2},{4,5},{5,4},{6,7},{7,6}} | collective-permute-start | bytes 100663304 | tf_op jit(solution)/shard_map/ppermute | solution.py:691

commit v7 on v6

--- a/solution.py
+++ b/solution.py
@@ -30,9 +30,9 @@
 
 def early_plan(s):
     n_down = jnp.where(s < 2, N_BLOCK, jnp.where(s == 2, 6, 0))
-    n_up = jnp.where(s == 0, 14, 0)
+    n_up = jnp.where(s == 0, 14, jnp.where(s == 1, 4, 0))
     after = jnp.where(s == 2, 12, 8)
-    each = jnp.where(s == 0, 60, jnp.where(s == 1, 5, 4))
+    each = jnp.where(s == 0, 60, jnp.where(s == 1, 16, 6))
     return n_down, n_up, after, each
 
 
@@ -125,7 +125,7 @@
 
     def ahead(k):
         is_f, _ = order(k)
-        return is_f & (first | (last & (k >= warm))) & (k < n_slot)
+        return is_f & (first | (k >= warm)) & (k < n_slot)
 
     def load_in(k):
         is_f, i = order(k)

time: 1220 us -> 1200 us (0.984)
  Pallas kernels: 1200 us -> 1170 us
    pallas_call x4, Pallas kernels: 273 us -> 259 us  [weight_grad(): pl.pallas_call(functools.partial(grad_kernel, up), out_shape=jax.ShapeDty...]
    pallas_call x1, Pallas kernels: 925 us -> 913 us  [run_pipeline(): pl.pallas_call(functools.partial(pipeline_kernel, n_stage, n_data, n_chun...]
where the time goes in v7:
time: 1200 us; the launch traced here: 1180 us
  Pallas kernels  1170 us (98%)
    pallas_call x1, Pallas kernels, run_pipeline(): pl.pallas_call(functools.partial(pipeline_kernel, n_stage, n_data, n_chun...  913 us
    pallas_call x4, Pallas kernels, weight_grad(): pl.pallas_call(functools.partial(grad_kernel, up), out_shape=jax.ShapeDty...  259 us
  transfers between devices with their start and end apart: 2, of which 0 were waited for; matrix products, arithmetic and copies ran while one was open for 0% of the time, Pallas kernels for 11%

profile of v7, /device:TPU:3, one launch (start us, length us, event | category | flops | bytes accessed | tf_op | source)
XLA Modules:
  0.0 1182.6 jit_solution(3411499741458682423)
XLA Ops:
  0.6 0.6 pad_add_fusion.sc
  1.3 912.6 %pipeline.1 = (bf16[4096,2048]{1,0:T(8,128)(2,1)}, bf16[4096,8192]{1,0:T(8,128)(2,1)}, f32[4096,8192]{1,0:T(8,128)}, bf16[4096,8192]{1,0:T(8,128)(2,1)}, bf16[40...) custom-call(bf16[4096,2048]{1,0:T(8,128)(2,1)} %bitcast.10, ...), custom_call_target="tpu_custom_call" | custom-call | flops 549755813888 | bytes 1073741824 | tf_op jit(solution)/shard_map/pipeline/pallas_call | solution.py:598
  913.8 73.2 %grad_up.2 = f32[1024,8192]{1,0:T(8,128)} custom-call(s32[2]{0:T(128)} %pad_add_fusion.sc, bf16[4096,2048]{1,0:T(8,128)(2,1)} %get-tuple-element.11.held, bf16[4096,8192]{1,0:T(8,128)(2,1)} %get-tuple-element.12.lo.hi, bf16[4096,8192]{1,0:T(8,128)(2,1)} %get-tuple-element.12.lo.hi, f32[2048,8192]{1,0:T(8,128)} %get-tuple-element.13.part), custom_call_target="tpu_custom_call" | custom-call | flops 68719476736 | bytes 134217728 | tf_op jit(solution)/shard_map/grad_up/pallas_call | solution.py:658
  987.1 5.0 collective-permute-start
  992.1 0.7 pad_add_fusion.3.sc
  992.7 0.0 copy-start
  992.7 51.1 %grad_down.2 = f32[8192,1024]{1,0:T(8,128)} custom-call(s32[2]{0:T(128)} %pad_add_fusion.3.sc, bf16[4096,2048]{1,0:T(8,128)(2,1)} %get-tuple-element.14.held, bf16[4096,8192]{1,0:T(8,128)(2,1)} %get-tuple-element.15.lo.hi, bf16[4096,8192]{1,0:T(8,128)(2,1)} %get-tuple-element.15.lo.hi, f32[8192,2048]{1,0:T(8,128)} %get-tuple-element.16.part), custom_call_target="tpu_custom_call" | custom-call | flops 68719476736 | bytes 134217728 | tf_op jit(solution)/shard_map/grad_down/pallas_call | solution.py:658
  1043.9 0.0 collective-permute-start.1
  1043.9 0.0 copy-done
  1043.9 0.6 reduce_sum.9
  1045.1 0.7 pad_add_fusion.1.sc
  1045.8 0.6 pad_add_fusion.2.sc
  1046.4 0.0 collective-permute-done.rest_0_
  1046.4 75.7 %grad_up.3 = f32[1024,8192]{1,0:T(8,128)} custom-call(s32[2]{0:T(128)} %pad_add_fusion.1.sc, bf16[4096,2048]{1,0:T(8,128)(2,1)} %get-tuple-element.11.held, bf16[4096,8192]{1,0:T(8,128)(2,1)} %get-tuple-element.12.lo.hi, bf16[4096,8192]{1,0:T(8,128)(2,1)} %get-tuple-element.12.lo.hi, f32[2048,8192]{1,0:T(8,128)} %get-tuple-element.13.part, ...), custom_call_target="tpu_custom_call" | custom-call | flops 68719476736 | bytes 134217728 | tf_op jit(solution)/shard_map/grad_up/pallas_call | solution.py:658
  1122.2 0.0 collective-permute-done.1.rest_0_
  1122.2 58.9 %grad_down.3 = f32[8192,1024]{1,0:T(8,128)} custom-call(s32[2]{0:T(128)} %pad_add_fusion.2.sc, bf16[4096,2048]{1,0:T(8,128)(2,1)} %get-tuple-element.14.held, bf16[4096,8192]{1,0:T(8,128)(2,1)} %get-tuple-element.15.lo.hi, bf16[4096,8192]{1,0:T(8,128)(2,1)} %get-tuple-element.15.lo.hi, f32[8192,2048]{1,0:T(8,128)} %get-tuple-element.16.part, ...), custom_call_target="tpu_custom_call" | custom-call | flops 68719476736 | bytes 134217728 | tf_op jit(solution)/shard_map/grad_down/pallas_call | solution.py:658
Async XLA Ops:
  987.1 59.4 %collective-permute-start = (f32[1024,8192]{1,0:T(8,128)}, f32[1024,8192]{1,0:T(8,128)}, u32[]{:S(2)}, u32[]{:S(2)}) collective-permute-start(f32[1024,8192]{1,0:T(8,128)} %grad_up.2), channel_id=1, source_target_pairs={{0,1},{1,0},{2,3},{3,2},{4,5},{5,4},{6,7},{7,6}} | collective-permute-start | bytes 100663304 | tf_op jit(solution)/shard_map/ppermute | solution.py:690
  992.7 51.1 %copy-start = (f32[8,512]{1,0:T(8,128)S(1)}, f32[8,512]{1,0:T(8,128)}, u32[]{:S(2)}) copy-start(f32[8,512]{1,0:T(8,128)} %get-tuple-element.10) | copy-start | bytes 49156
  1043.9 78.3 %collective-permute-start.1 = (f32[8192,1024]{1,0:T(8,128)}, f32[8192,1024]{1,0:T(8,128)}, u32[]{:S(2)}, u32[]{:S(2)}) collective-permute-start(f32[8192,1024]{1,0:T(8,128)} %grad_down.2), channel_id=1, source_target_pairs={{0,1},{1,0},{2,3},{3,2},{4,5},{5,4},{6,7},{7,6}} | collective-permute-start | bytes 100663304 | tf_op jit(solution)/shard_map/ppermute | solution.py:691

commit v8 on v7

--- a/solution.py
+++ b/solution.py
@@ -29,10 +29,10 @@
 
 
 def early_plan(s):
-    n_down = jnp.where(s < 2, N_BLOCK, jnp.where(s == 2, 6, 0))
-    n_up = jnp.where(s == 0, 14, jnp.where(s == 1, 4, 0))
+    n_down = jnp.where(s < 2, N_BLOCK, jnp.where(s == 2, 8, 0))
+    n_up = jnp.where(s == 0, 14, jnp.where(s == 1, 2, 0))
     after = jnp.where(s == 2, 12, 8)
-    each = jnp.where(s == 0, 60, jnp.where(s == 1, 16, 6))
+    each = jnp.where(s == 0, 60, jnp.where(s == 1, 16, 8))
     return n_down, n_up, after, each
 
 
@@ -286,11 +286,16 @@
 
             @pl.when(last)
             def _():
-                for j in (2 * jj, 2 * jj + 1):
-                    for r in range(0, ROWS, 16):
-                        diff = out[o, pl.ds(r, 16), cols(j, DT)].astype(F32) - inb[1 - p, pl.ds(r, 16), cols(j, DT)].astype(F32)
-                        loss_acc[...] += diff * diff
-                        inb[1 - p, pl.ds(r, 16), cols(j, DT)] = (diff * inv_total).astype(BF16)
+                def pieces(c, carry):
+                    for j in (2 * jj, 2 * jj + 1):
+                        for z in range(0, 32, 16):
+                            r = pl.ds(pl.multiple_of(c * 32 + z, 16), 16)
+                            diff = out[o, r, cols(j, DT)].astype(F32) - inb[1 - p, r, cols(j, DT)].astype(F32)
+                            loss_acc[...] += diff * diff
+                            inb[1 - p, r, cols(j, DT)] = (diff * inv_total).astype(BF16)
+                    return carry
+
+                lax.fori_loop(0, ROWS // 32, pieces, 0)
 
         wait_d(2)
 
@@ -323,12 +328,14 @@
             wait_d(d_in_slot(j, 0))
             wait_d(d_in_slot(j, 1))
             wait_ring(j)
-            pa = dot(inb[p], w2r[cols(j, CT), :], NT).astype(BF16).astype(F32)
-            gq[:, d_cols(j, 0)] = (pa * dbuf[d_in_slot(j, 0)]).astype(BF16)
-            pb = dot(inb[p, :, pl.ds(0, CT)], ring[j, pl.ds(0, CT)], NT)
-            pb = pb + dot(inb[p, :, pl.ds(CT, CT)], ring[j, pl.ds(CT, CT)], NT)
-            pb = pb.astype(BF16).astype(F32)
-            gq[:, d_cols(j, 1)] = (pb * dbuf[d_in_slot(j, 1)]).astype(BF16)
+            for z in range(2):
+                pa = dot(inb[p], w2r[cols(2 * j + z, DT), :], NT).astype(BF16).astype(F32)
+                gq[:, cols(2 * j + z, DT)] = (pa * dbuf[d_in_slot(j, 0), :, pl.ds(z * DT, DT)]).astype(BF16)
+            for z in range(2):
+                pb = dot(inb[p, :, pl.ds(0, CT)], ring[j, pl.ds(z * DT, DT)], NT)
+                pb = pb + dot(inb[p, :, pl.ds(CT, CT)], ring[j, pl.ds(CT + z * DT, DT)], NT)
+                pb = pb.astype(BF16).astype(F32)
+                gq[:, cols(2 * j + z, DT, half)] = (pb * dbuf[d_in_slot(j, 1), :, pl.ds(z * DT, DT)]).astype(BF16)
             for b in range(2):
                 copy(gq.at[:, d_cols(j, b)], qs.at[rows(i), d_cols(j, b)], gq_sem).start()
             return carry
@@ -433,7 +440,7 @@
                 copy(ring.at[2], ring.at[2], held_sem).wait()
 
             tile(u, False)
-            for z in range(2):
+            def half_unit(z, carry):
                 t = 2 * (u - lo) + z
                 q = part_slot(t)
 
@@ -450,10 +457,13 @@
                 def _():
                     for a in range(2):
                         r = 2 * z + a
-                        dbuf[q, :, pl.ds(a * DT, DT)] = dot(ring[2, :, pl.ds(r * ROWS, ROWS)], ring[3, :, pl.ds(pl.multiple_of(c0, DT), DT)], TN)
+                        dbuf[q, :, pl.ds(a * DT, DT)] = dot(ring[2, :, cols(r, ROWS)], ring[3, :, pl.ds(pl.multiple_of(c0, DT), DT)], TN)
                     for a in range(2):
                         r = 2 * z + a
                         copy(dbuf.at[q, :, pl.ds(a * DT, DT)], up_part.at[cols(4 * hf + r, ROWS), cols(b, DT)], part_sem.at[lax.rem(t, 3)]).start()
+                return carry
+
+            lax.fori_loop(0, 2, half_unit, 0)
             return carry
 
         lax.fori_loop(lo, hi, unit, 0)

time: 1200 us -> 1190 us (level); the launches traced: 1180 us -> 1190 us
  no operation moved by 1% of the time
where the time goes in v8:
time: 1190 us
  Pallas kernels  1170 us (98%)
    pallas_call x1, Pallas kernels, run_pipeline(): pl.pallas_call(functools.partial(pipeline_kernel, n_stage, n_data, n_chun...  909 us
    pallas_call x4, Pallas kernels, weight_grad(): pl.pallas_call(functools.partial(grad_kernel, up), out_shape=jax.ShapeDty...  265 us
  transfers between devices with their start and end apart: 2, of which 0 were waited for; matrix products, arithmetic and copies ran while one was open for 0% of the time, Pallas kernels for 11%

profile of v8, /device:TPU:3, one launch (start us, length us, event | category | flops | bytes accessed | tf_op | source)
XLA Modules:
  0.0 1186.4 jit_solution(14052564463380502028)
XLA Ops:
  0.6 0.6 pad_add_fusion.sc
  1.3 909.2 %pipeline.1 = (bf16[4096,2048]{1,0:T(8,128)(2,1)}, bf16[4096,8192]{1,0:T(8,128)(2,1)}, f32[4096,8192]{1,0:T(8,128)}, bf16[4096,8192]{1,0:T(8,128)(2,1)}, bf16[40...) custom-call(bf16[4096,2048]{1,0:T(8,128)(2,1)} %bitcast.10, ...), custom_call_target="tpu_custom_call" | custom-call | flops 549755813888 | bytes 1073741824 | tf_op jit(solution)/shard_map/pipeline/pallas_call | solution.py:608
  910.4 76.9 %grad_up.2 = f32[1024,8192]{1,0:T(8,128)} custom-call(s32[2]{0:T(128)} %pad_add_fusion.sc, bf16[4096,2048]{1,0:T(8,128)(2,1)} %get-tuple-element.11.held, bf16[4096,8192]{1,0:T(8,128)(2,1)} %get-tuple-element.12.lo.hi, bf16[4096,8192]{1,0:T(8,128)(2,1)} %get-tuple-element.12.lo.hi, f32[2048,8192]{1,0:T(8,128)} %get-tuple-element.13.part), custom_call_target="tpu_custom_call" | custom-call | flops 68719476736 | bytes 134217728 | tf_op jit(solution)/shard_map/grad_up/pallas_call | solution.py:668
  987.3 6.2 collective-permute-start
  993.6 0.7 pad_add_fusion.3.sc
  994.2 0.0 copy-start
  994.2 51.1 %grad_down.2 = f32[8192,1024]{1,0:T(8,128)} custom-call(s32[2]{0:T(128)} %pad_add_fusion.3.sc, bf16[4096,2048]{1,0:T(8,128)(2,1)} %get-tuple-element.14.held, bf16[4096,8192]{1,0:T(8,128)(2,1)} %get-tuple-element.15.lo.hi, bf16[4096,8192]{1,0:T(8,128)(2,1)} %get-tuple-element.15.lo.hi, f32[8192,2048]{1,0:T(8,128)} %get-tuple-element.16.part), custom_call_target="tpu_custom_call" | custom-call | flops 68719476736 | bytes 134217728 | tf_op jit(solution)/shard_map/grad_down/pallas_call | solution.py:668
  1045.4 0.0 collective-permute-start.1
  1045.4 0.0 copy-done
  1045.4 0.6 reduce_sum.9
  1046.6 0.7 pad_add_fusion.1.sc
  1047.3 0.6 pad_add_fusion.2.sc
  1048.0 0.0 collective-permute-done.rest_0_
  1048.0 78.4 %grad_up.3 = f32[1024,8192]{1,0:T(8,128)} custom-call(s32[2]{0:T(128)} %pad_add_fusion.1.sc, bf16[4096,2048]{1,0:T(8,128)(2,1)} %get-tuple-element.11.held, bf16[4096,8192]{1,0:T(8,128)(2,1)} %get-tuple-element.12.lo.hi, bf16[4096,8192]{1,0:T(8,128)(2,1)} %get-tuple-element.12.lo.hi, f32[2048,8192]{1,0:T(8,128)} %get-tuple-element.13.part, ...), custom_call_target="tpu_custom_call" | custom-call | flops 68719476736 | bytes 134217728 | tf_op jit(solution)/shard_map/grad_up/pallas_call | solution.py:668
  1126.4 0.0 collective-permute-done.1.rest_0_
  1126.4 58.9 %grad_down.3 = f32[8192,1024]{1,0:T(8,128)} custom-call(s32[2]{0:T(128)} %pad_add_fusion.2.sc, bf16[4096,2048]{1,0:T(8,128)(2,1)} %get-tuple-element.14.held, bf16[4096,8192]{1,0:T(8,128)(2,1)} %get-tuple-element.15.lo.hi, bf16[4096,8192]{1,0:T(8,128)(2,1)} %get-tuple-element.15.lo.hi, f32[8192,2048]{1,0:T(8,128)} %get-tuple-element.16.part, ...), custom_call_target="tpu_custom_call" | custom-call | flops 68719476736 | bytes 134217728 | tf_op jit(solution)/shard_map/grad_down/pallas_call | solution.py:668
Async XLA Ops:
  987.3 60.6 %collective-permute-start = (f32[1024,8192]{1,0:T(8,128)}, f32[1024,8192]{1,0:T(8,128)}, u32[]{:S(2)}, u32[]{:S(2)}) collective-permute-start(f32[1024,8192]{1,0:T(8,128)} %grad_up.2), channel_id=1, source_target_pairs={{0,1},{1,0},{2,3},{3,2},{4,5},{5,4},{6,7},{7,6}} | collective-permute-start | bytes 100663304 | tf_op jit(solution)/shard_map/ppermute | solution.py:700
  994.2 51.1 %copy-start = (f32[8,512]{1,0:T(8,128)S(1)}, f32[8,512]{1,0:T(8,128)}, u32[]{:S(2)}) copy-start(f32[8,512]{1,0:T(8,128)} %get-tuple-element.10) | copy-start | bytes 49156
  1045.4 81.0 %collective-permute-start.1 = (f32[8192,1024]{1,0:T(8,128)}, f32[8192,1024]{1,0:T(8,128)}, u32[]{:S(2)}, u32[]{:S(2)}) collective-permute-start(f32[8192,1024]{1,0:T(8,128)} %grad_down.2), channel_id=1, source_target_pairs={{0,1},{1,0},{2,3},{3,2},{4,5},{5,4},{6,7},{7,6}} | collective-permute-start | bytes 100663304 | tf_op jit(solution)/shard_map/ppermute | solution.py:701
